TPU v7x, 32 devices: a whole 2x2x4 slice. The times are simulated.
32 devices in a mesh: model: 4 (over z), sub: 2 (over y), data: 4 (over x, core).
Axes of the slice: x: 2, y: 2, z: 4, core: 2. Of those that a mesh axis runs over, the one named last changes fastest.
Arguments:
- images: bfloat16 [256, 196, 512], P(('model', 'sub', 'data'))
- targets: bfloat16 [256, 196, 512], P(('model', 'sub', 'data'))
- w_in: float32 [4, 512, 2048], replicated
- w_out: float32 [4, 2048, 512], replicated
Outputs:
- output 1: float32 [4, 512, 2048], replicated
- output 2: float32 [4, 2048, 512], replicated
- output 3: float32 [], replicated
All inputs are finite; a program needn't handle non-finite values.
Results may differ from a plain program's by a relative error of at most 0.00108718.
Values are sent between devices in bfloat16 or wider.
A program may use at most 1 GiB of HBM per device.

v0:
```python
import jax
import jax.numpy as jnp
import math
from jax import lax
from jax.sharding import PartitionSpec as P

RHO_REL = 0.1
LEARN_RATE = 8.0
SQRT_HALF = 0.7071067811865476
INV_SQRT_2PI = 0.3989422804014327


def gelu_fn(pre_act):
    return 0.5 * pre_act * (1.0 + lax.erf(pre_act * SQRT_HALF))


def gelu_slope(pre_act):
    cdf_part = 0.5 * (1.0 + lax.erf(pre_act * SQRT_HALF))
    return cdf_part + pre_act * INV_SQRT_2PI * jnp.exp(-0.5 * pre_act * pre_act)


def forward(x_rows, in_list, out_list):
    hidden = x_rows
    saved_acts = []
    for layer_idx in range(len(in_list)):
        pre_act = jnp.dot(hidden, in_list[layer_idx], preferred_element_type=jnp.float32).astype(jnp.bfloat16)
        post_act = gelu_fn(pre_act.astype(jnp.float32)).astype(jnp.bfloat16)
        mlp_out = jnp.dot(post_act, out_list[layer_idx], preferred_element_type=jnp.float32)
        saved_acts.append((hidden, pre_act, post_act))
        hidden = (hidden.astype(jnp.float32) + mlp_out).astype(jnp.bfloat16)
    return hidden, saved_acts


def backward(d_top, saved_acts, in_list, out_list):
    d_hidden = d_top
    grads_in = []
    grads_out = []
    for layer_idx in reversed(range(len(saved_acts))):
        hidden, pre_act, post_act = saved_acts[layer_idx]
        grads_out.append(jnp.einsum('tf,td->fd', post_act, d_hidden, preferred_element_type=jnp.float32))
        d_act = jnp.einsum('td,fd->tf', d_hidden, out_list[layer_idx], preferred_element_type=jnp.float32)
        d_pre = (d_act * gelu_slope(pre_act.astype(jnp.float32))).astype(jnp.bfloat16)
        grads_in.append(jnp.einsum('td,tf->df', hidden, d_pre, preferred_element_type=jnp.float32))
        if layer_idx > 0:
            back_part = jnp.einsum('tf,df->td', d_pre, in_list[layer_idx], preferred_element_type=jnp.float32)
            d_hidden = (d_hidden.astype(jnp.float32) + back_part).astype(jnp.bfloat16)
    return grads_in[::-1], grads_out[::-1]


def top_grad(top_hidden, y_rows, inv_count):
    resid_err = top_hidden.astype(jnp.float32) - y_rows.astype(jnp.float32)
    return 0.5 * jnp.sum(resid_err * resid_err), (resid_err * inv_count).astype(jnp.bfloat16)


def solution(mesh):
    mesh_axes = tuple(mesh.axis_names)
    dev_count = math.prod([mesh.shape[axis_name] for axis_name in mesh_axes])
    batch_spec = P(mesh_axes, None, None)

    def local_step(images, targets, w_in, w_out):
        layers, model_dim, hidden_dim = w_in.shape
        tok_local = images.shape[0] * images.shape[1]
        inv_count = 1.0 / (tok_local * dev_count * model_dim)
        radius = RHO_REL * math.sqrt(layers * hidden_dim + model_dim)
        x_rows = images.reshape(tok_local, model_dim)
        y_rows = targets.reshape(tok_local, model_dim)
        w_in_bf = w_in.astype(jnp.bfloat16)
        w_out_bf = w_out.astype(jnp.bfloat16)
        in_list = [w_in_bf[layer_idx] for layer_idx in range(layers)]
        out_list = [w_out_bf[layer_idx] for layer_idx in range(layers)]
        top_hidden, saved_acts = forward(x_rows, in_list, out_list)
        _, d_top = top_grad(top_hidden, y_rows, inv_count)
        grads_in, grads_out = backward(d_top, saved_acts, in_list, out_list)
        grads_in, grads_out = lax.psum((grads_in, grads_out), mesh_axes)
        norm_sq = sum(jnp.sum(grad_part * grad_part) for grad_part in grads_in + grads_out)
        step_scale = radius / jnp.sqrt(norm_sq)
        pert_in = [(w_in[layer_idx] + step_scale * grads_in[layer_idx]).astype(jnp.bfloat16) for layer_idx in range(layers)]
        pert_out = [(w_out[layer_idx] + step_scale * grads_out[layer_idx]).astype(jnp.bfloat16) for layer_idx in range(layers)]
        top_pert, saved_pert = forward(x_rows, pert_in, pert_out)
        loss_local, d_pert = top_grad(top_pert, y_rows, inv_count)
        grads2_in, grads2_out = backward(d_pert, saved_pert, pert_in, pert_out)
        grads2_in, grads2_out, loss_total = lax.psum((grads2_in, grads2_out, loss_local), mesh_axes)
        new_in = w_in - LEARN_RATE * jnp.stack(grads2_in)
        new_out = w_out - LEARN_RATE * jnp.stack(grads2_out)
        return new_in, new_out, loss_total * inv_count

    return jax.shard_map(local_step, mesh=mesh, in_specs=(batch_spec, batch_spec, P(), P()), out_specs=(P(), P(), P()), check_vma=False)
```

profile of v0, /device:TPU:0, one launch (start us, length us, event | category | flops | bytes accessed | tf_op | source)
XLA Modules:
  0.0 1572.3 jit_solution(6643580191584641490)
XLA Ops:
  7.2 2.0 copy.21
  9.3 1.3 reshape.12
  10.6 2.2 copy.23
  12.8 2.1 reshape.13
  15.0 7.6 convert_element_type.244
  22.6 9.6 convert_element_type.240
  32.3 9.3 fusion.10
  41.5 11.9 fusion.86
  53.5 9.4 fusion.19
  62.8 11.9 add_convert_fusion.11
  74.7 9.4 fusion.28
  84.1 11.9 add_convert_fusion.10
  96.0 8.0 fusion.37
  104.1 9.2 multiply_convert_fusion.1
  113.3 9.8 fusion.104
  123.0 10.1 fusion.41
  133.1 7.2 add_convert_fusion.8
  140.4 5.6 fusion.118
  145.9 13.2 fusion.107
  159.1 12.2 fusion.32
  171.3 7.2 add_convert_fusion.7
  178.5 10.5 fusion.117
  189.1 12.9 fusion.110
  202.0 12.0 fusion.23
  214.0 7.7 add_convert_fusion.6
  221.7 18.7 %convolution_bitcast_fusion.8 = f32[512,2048]{0,1:T(8,128)} fusion(bf16[1568,512]{1,0:T(8,128)(2,1)} %reshape.12, bf16[1568,2048]{1,0:T(8,128)(2,1)} %get-tuple-element.33, f32[1568,2048]{1,0:T(8,128)} %get-tuple-element.32, bf16[1568,512]{1,0:T(8,128)(2,1)} %add_convert_fusion.6, bf16[4,2048,512]{2,1,0:T(8,128)(2,1)} %copy-done.7), kind=kOutput, calls=%fused_computation.161 | convolution fusion | flops 6605570048 | bytes 28770304 | tf_op jit(solution)/shard_map/td,tf->df/dot_general | solution.py:43
  240.4 13.0 fusion.113
  253.5 5.6 fusion.116
  259.2 16.5 %copy.33 = f32[4,512,2048]{1,2,0:T(8,128)} copy(f32[4,512,2048]{2,1,0:T(8,128)} %param.6) | data formatting | bytes 33554432 | tf_op args[2]
  275.7 484.6 %all-reduce.7.cloned.1.call-done = (f32[2048,512]{1,0:T(8,128)}, f32[512,2048]{0,1:T(8,128)}, f32[512,2048]{0,1:T(8,128)}, f32[512,2048]{0,1:T(8,128)}, f32[512,...) async-done(((f32[2048,512]{1,0:T(8,128)}, f32[512,2048]{0,1:T(8,128)}, f32[512,2048]{0,1:T(8,128)}, f32[512,2048]{0,1:T(8,128)}, ...) | async-done | bytes 33554448 | tf_op jit(solution)/shard_map/psum | solution.py:74
  760.3 5.4 multiply_reduce_fusion.2
  765.7 0.5 copy-done.5
  766.2 1.7 multiply_reduce_fusion.6
  769.2 5.2 multiply_reduce_fusion.4
  776.9 5.2 multiply_reduce_fusion
  783.4 16.2 %fusion.82 = (bf16[2048,512]{1,0:T(8,128)(2,1)}, bf16[2048,512]{1,0:T(8,128)(2,1)}, bf16[2048,512]{1,0:T(8,128)(2,1)}, bf16[2048,512]{1,0:T(8,128)(2,1)}) fusion(f32[2048,512]{1,0:T(8,128)} %get-tuple-element.24, f32[4,2048,512]{2,1,0:T(8,128)} %param.7, f32[]{:T(128)S(6)} %div.3, f32[2048,512]{1,0:T(8,128)} %get-tuple-element.23, ...), kind=kLoop, calls=%fused_computation.136 | loop fusion | flops 12582912 | bytes 41943044 | tf_op jit(solution)/shard_map/convert_element_type | solution.py:78
  799.6 11.4 fusion.75
  811.0 8.5 fusion.73
  819.6 11.3 fusion.87
  831.0 6.7 fusion.46
  837.6 10.8 add_convert_fusion.5
  848.5 6.9 fusion.55
  855.4 11.3 add_convert_fusion.4
  866.7 8.3 fusion.64
  875.0 9.0 multiply_reduce_fusion.8
  884.0 10.0 convolution_bitcast_fusion
  894.0 10.2 fusion.68
  904.2 7.2 add_convert_fusion.2
  911.5 5.6 convolution_bitcast_fusion.4
  917.1 13.1 convolution_bitcast_fusion.1
  930.2 10.5 fusion.59
  940.8 6.9 add_convert_fusion.1
  947.8 5.8 convolution_bitcast_fusion.5
  953.6 10.0 convolution_bitcast_fusion.2
  963.6 10.5 fusion.50
  974.1 6.9 add_convert_fusion
  981.1 5.6 convolution_bitcast_fusion.6
  986.7 14.7 convolution_bitcast_fusion.7
  1001.4 12.8 convolution_bitcast_fusion.3
  1014.9 40.5 %psum.135 = f32[]{:T(128)} all-reduce(f32[]{:T(128)S(6)} %mul.408), channel_id=1, replica_groups=mesh['model'=4,'sub'=2,'data'=4] {'model','sub','data'}, use_global_device_ids=true, to_apply=%region_25.0 | all-reduce | flops 1 | bytes 8 | tf_op jit(solution)/shard_map/psum | solution.py:82
  1056.0 456.9 %all-reduce.5.cloned.1.call-done = (f32[1,512,2048]{1,2,0:T(8,128)}, f32[1,512,2048]{1,2,0:T(8,128)}, f32[1,512,2048]{1,2,0:T(8,128)}, f32[1,512,2048]{1,2,0:T(8...) async-done(((f32[1,512,2048]{1,2,0:T(8,128)}, f32[1,512,2048]{1,2,0:T(8,128)}, ...) | async-done | bytes 33554448 | tf_op jit(solution)/shard_map/psum | solution.py:82
  1512.9 17.3 %fusion = f32[4,512,2048]{1,2,0:T(8,128)} fusion(f32[4,512,2048]{1,2,0:T(8,128)} %copy.33, f32[1,512,2048]{1,2,0:T(8,128)} %get-tuple-element.9, f32[1,512,2048]{1,2,0:T(8,128)} %get-tuple-element.10, f32[1,512,2048]{1,2,0:T(8,128)} %get-tuple-element.11, f32[1,512,2048]{1,2,0:T(8,128)} %get-tuple-element.12), kind=kLoop, calls=%fused_computation.37 | loop fusion | flops 20971520 | bytes 50331648 | tf_op jit(solution)/shard_map/sub | solution.py:83
  1530.2 16.3 %copy.34 = f32[4,512,2048]{2,1,0:T(8,128)} copy(f32[4,512,2048]{1,2,0:T(8,128)} %fusion) | data formatting | bytes 33554432
  1546.5 17.3 %fusion.1 = f32[4,2048,512]{2,1,0:T(8,128)} fusion(f32[4,2048,512]{2,1,0:T(8,128)} %param.7, f32[1,2048,512]{2,1,0:T(8,128)} %get-tuple-element.13, f32[1,2048,512]{2,1,0:T(8,128)} %get-tuple-element.14, f32[1,2048,512]{2,1,0:T(8,128)} %get-tuple-element.15, f32[1,2048,512]{2,1,0:T(8,128)} %get-tuple-element.16), kind=kLoop, calls=%fused_computation.39 | loop fusion | flops 20971520 | bytes 50331648 | tf_op jit(solution)/shard_map/sub | solution.py:84
  (119 shorter events, 0.3 us)
Async XLA Ops:
  7.2 3.4 copy-start.25
  7.2 753.1 %all-reduce.7.cloned.1.call-start = ((), (), s32[]{:S(2)}) async-start(), calls=%async_computation.1 | async-start | bytes 67108864 | tf_op jit(solution)/shard_map/psum | solution.py:74
  14.9 89.1 %copy-start = (f32[1568,512]{1,0:T(8,128)}, f32[1568,512]{1,0:T(8,128)S(1)}, u32[]{:S(2)}) copy-start(f32[1568,512]{1,0:T(8,128)S(1)} %reshape.13) | copy-start | bytes 9633796
  22.6 61.5 %copy-start.7 = (bf16[4,2048,512]{2,1,0:T(8,128)(2,1)}, bf16[4,2048,512]{2,1,0:T(8,128)(2,1)S(1)}, u32[]{:S(2)}) copy-start(bf16[4,2048,512]{2,1,0:T(8,128)(2,1)S(1)} %convert_element_type.244) | copy-start | bytes 25165828
  22.6 9.6 copy-start.9
  32.2 42.5 %copy-start.8 = (bf16[4,512,2048]{2,1,0:T(8,128)(2,1)}, bf16[4,512,2048]{2,1,0:T(8,128)(2,1)S(1)}, u32[]{:S(2)}) copy-start(bf16[4,512,2048]{2,1,0:T(8,128)(2,1)S(1)} %convert_element_type.240) | copy-start | bytes 25165828
  113.3 9.8 copy-start.13
  133.1 7.2 copy-start.12
  133.1 7.2 copy-start.43
  140.3 5.6 copy-start.35
  140.4 18.7 %slice-start = ((s8[8388608]{0:T(1024)(128)(4,1)}), s8[4194304]{0:T(1024)(128)(4,1)S(1)}, s32[]{:S(2)}) async-start(s8[8388608]{0:T(1024)(128)(4,1)} %bitcast.178), calls=%async_computation.2 | async-start | bytes 8388608
  145.9 13.2 slice-start.1
  145.9 25.4 %slice-start.2 = ((s8[8388608]{0:T(1024)(128)(4,1)}), s8[4194304]{0:T(1024)(128)(4,1)S(1)}, s32[]{:S(2)}) async-start(s8[8388608]{0:T(1024)(128)(4,1)} %bitcast.180), calls=%async_computation.4 | async-start | bytes 8388608
  159.1 12.2 slice-start.3
  171.3 7.2 copy-start.33
  178.5 10.5 copy-start.34
  221.7 18.7 %copy-start.36 = (bf16[1568,512]{1,0:T(8,128)(2,1)S(1)}, bf16[1568,512]{1,0:T(8,128)(2,1)}, u32[]{:S(2)}) copy-start(bf16[1568,512]{1,0:T(8,128)(2,1)} %add_convert_fusion.6) | copy-start | bytes 4816900
  240.4 13.1 copy-start.32
  240.4 13.1 copy-start.39
  259.1 1253.7 %all-reduce.5.cloned.1.call-start = ((), (), s32[]{:S(2)}) async-start(), calls=%async_computation | async-start | bytes 67108864 | tf_op jit(solution)/shard_map/psum | solution.py:82
  760.3 5.4 copy-start.3
  760.3 5.9 copy-start.5
  783.4 16.3 %copy-start.6 = (f32[512,2048]{0,1:T(8,128)S(1)}, f32[512,2048]{0,1:T(8,128)}, u32[]{:S(2)}) copy-start(f32[512,2048]{0,1:T(8,128)} %get-tuple-element.19) | copy-start | bytes 12582916
  799.6 11.4 copy-start.4
  811.0 8.5 copy-start.10
  811.0 8.5 copy-start.16
  819.5 11.4 copy-start.2
  819.6 11.4 copy-start.19
  830.9 6.7 copy-start.28
  831.0 6.7 copy-start.17
  837.6 10.8 copy-start.27
  837.6 10.8 copy-start.23
  848.5 7.0 copy-start.30
  848.5 6.9 copy-start.21
  855.4 11.3 copy-start.26
  866.7 8.3 copy-start.14
  866.7 8.3 copy-start.1
  904.2 7.2 copy-start.15
  904.2 7.2 copy-start.40
  911.4 5.6 copy-start.37
  911.5 18.7 %slice-start.8 = ((s8[12845056]{0:T(1024)(128)(4,1)}), s8[4194304]{0:T(1024)(128)(4,1)S(1)}, s32[]{:S(2)}) async-start(s8[12845056]{0:T(1024)(128)(4,1)} %bitcast.184), calls=%async_computation.10 | async-start | bytes 8388608
  911.5 18.7 %slice-start.9 = ((s8[12845056]{0:T(1024)(128)(4,1)}), s8[4194304]{0:T(1024)(128)(4,1)S(1)}, s32[]{:S(2)}) async-start(s8[12845056]{0:T(1024)(128)(4,1)} %bitcast.184), calls=%async_computation.11 | async-start | bytes 8388608
  917.0 13.1 copy-start.22
  917.0 13.1 slice-start.10
  917.1 13.1 slice-start.11
  930.2 10.5 copy-start.24
  940.7 7.0 copy-start.31
  940.7 7.0 copy-start.41
  940.7 12.8 slice-start.4
  940.7 12.8 slice-start.5
  940.8 12.8 slice-start.6
  947.7 5.8 copy-start.38
  947.8 5.8 slice-start.7
  953.6 10.0 copy-start.18
  963.6 10.5 copy-start.20
  974.1 7.0 copy-start.29
  974.1 7.0 copy-start.42
  981.1 5.6 copy-start.11
Sparse Core Ops, SparseCore 0:
  259.2 500.9 all-reduce.6
  1014.3 498.4 all-reduce.4
where the time goes:
time: 1580 us; the launch traced here: 1570 us
  waiting for transfers between devices  942 us (60%)
  matrix products  429 us (27%)
  other arithmetic  96.9 us (6%)
  local copies, waits for them, and re-layouts  41.2 us (3%)
  blocking collectives  40.5 us (3%)
  between operations  22.8 us (1%)
    psum x1, waiting for transfers between devices, local_step(): grads_in, grads_out = lax.psum((grads_in, grads_out), mesh_axes)  485 us
    psum x1, waiting for transfers between devices, local_step(): lax.psum((grads2_in, grads2_out, loss_local), mesh_axes)  457 us
    dot_general x8, matrix products, backward(): jnp.einsum('tf,td->fd', post_act, d_hidden, preferred_element_type=jnp.fl...  94.8 us
    dot_general x8, matrix products, forward(): jnp.dot(post_act, out_list[layer_idx], preferred_element_type=jnp.float32)  87.3 us
    dot_general x8, matrix products, backward(): jnp.einsum('td,tf->df', hidden, d_pre, preferred_element_type=jnp.float32)  72 us
    dot_general x8, matrix products, forward(): jnp.dot(hidden, in_list[layer_idx], preferred_element_type=jnp.float32)  66.4 us
    dot_general x6, matrix products, backward(): jnp.einsum('td,fd->tf', d_hidden, out_list[layer_idx], preferred_element_...  65.5 us
    dot_general x6, matrix products, backward(): jnp.einsum('tf,df->td', d_pre, in_list[layer_idx], preferred_element_type...  43.2 us
  transfers between devices with their start and end apart: 2, of which 2 were waited for; matrix products, arithmetic and copies ran while one was open for 1% of the time, Pallas kernels for 0%

commit v1 on v0

v1 whole, which is shorter than its diff:
```python
import math

import jax
import jax.numpy as jnp
from jax import lax
from jax.experimental import pallas as pl
from jax.experimental.pallas import tpu as pltpu
from jax.sharding import PartitionSpec as P

MESH = pl.DeviceIdType.MESH
f32 = jnp.float32
bf16 = jnp.bfloat16
RHO_REL = 0.1
LEARN_RATE = 8.0
SQRT_HALF = 0.7071067811865476
INV_SQRT_PI = 0.5641895835477563
LOG2_E = 1.4426950408889634
LAYERS, D, F = 4, 512, 2048
HALF = F // 2
W = 256
NU = 32
ROWS = (512, 256, 128, 64, 32)
VMEM_LIMIT = 62 * 2**20

ANY = pl.BlockSpec(memory_space=pl.ANY)
DMA = pltpu.SemaphoreType.DMA


def aligned(value, multiple):
    return pl.multiple_of(value, multiple)


def gelu(x):
    return (0.5 * x) * (1.0 + lax.erf(x * SQRT_HALF))


def gelu_slope(x):
    z = x * SQRT_HALF
    return (0.5 + 0.5 * lax.erf(z)) + (z * INV_SQRT_PI) * jnp.exp2(z * z * (-LOG2_E))


def coords():
    z, y, dd = lax.axis_index("model"), lax.axis_index("sub"), lax.axis_index("data")
    return z, y, dd // 2, dd % 2


class Cube:
    def __init__(self):
        z, y, x, c = coords()
        fx, fy = 1 - 2 * x, 1 - 2 * y
        self.core = c
        self.devs = (
            (z, y, x * 2 + (1 - c)),
            (z, y + c * fy, (x + (1 - c) * fx) * 2 + c),
            (z + 1 - 2 * (z % 2), y, x * 2 + c),
            (z, y + (1 - c) * fy, (x + c * fx) * 2 + c),
            ((z + 2) % 4, y, x * 2 + c),
        )
        bits = (x * (1 - c) + y * c, z % 2, y * (1 - c) + x * c, z // 2)
        self.keep, self.give, base = [], [], 0
        for i in range(4):
            half = ROWS[i + 1]
            self.keep.append(base + bits[i] * half)
            self.give.append(base + (1 - bits[i]) * half)
            base = base + bits[i] * half

    def barrier(self):
        sem = pltpu.get_barrier_semaphore()
        for dev in self.devs:
            pl.semaphore_signal(sem, inc=1, device_id=dev, device_id_type=MESH)
        pl.semaphore_wait(sem, len(self.devs))


def remote(src, dst, send_sem, recv_sem, dev):
    return pltpu.make_async_remote_copy(
        src_ref=src, dst_ref=dst, send_sem=send_sem, recv_sem=recv_sem, device_id=dev, device_id_type=MESH
    )


class ReduceScatter:
    NSD, ND, NA, N, LAG = 4, 8, 16, 8, 2
    TICKS = NU + 4 * LAG

    @classmethod
    def scratch(cls):
        n = cls.N
        return [
            pltpu.VMEM((cls.NSD, 512, W), f32),
            pltpu.VMEM((cls.NA, 512, W), f32),
            pltpu.VMEM((cls.ND, 512, W), f32),
            pltpu.VMEM((n, 256, W), f32),
            pltpu.VMEM((n, 128, W), f32),
            pltpu.VMEM((n, 64, W), f32),
            pltpu.VMEM((n, 32, W), f32),
            DMA((cls.NSD,)),
            DMA((cls.ND,)),
            DMA((4, n)),
            DMA((4, n)),
            pltpu.SemaphoreType.REGULAR,
        ]

    def __init__(self, cube, refs):
        self.cube = cube
        (self.out, self.acc, self.inc, r1, r2, r3, r4, self.dsend, self.drecv, self.ssem, self.rsem, self.credit) = refs
        self.recv = (r1, r2, r3, r4)

    def core_copy(self, k):
        return remote(
            self.out.at[k % self.NSD],
            self.inc.at[k % self.ND],
            self.dsend.at[k % self.NSD],
            self.drecv.at[k % self.ND],
            self.cube.devs[0],
        )

    def copy(self, i, k):
        n = ROWS[i + 1]
        return remote(
            self.acc.at[k % self.NA, pl.ds(aligned(self.cube.give[i], n), n), :],
            self.recv[i].at[k % self.N],
            self.ssem.at[i, k % self.N],
            self.rsem.at[i, k % self.N],
            self.cube.devs[i + 1],
        )

    def before_write(self, k):
        @pl.when(k >= self.NSD)
        def _():
            self.core_copy(k - self.NSD).wait_send()

    def push(self, k):
        @pl.when(k >= self.ND)
        def _():
            pl.semaphore_wait(self.credit, 1)

        self.core_copy(k).start()

    def finish(self):
        for k in range(NU - self.NSD, NU):
            self.core_copy(k).wait_send()
        pl.semaphore_wait(self.credit, self.ND)

    def tick(self, t, final):
        @pl.when((t >= 0) & (t < NU))
        def _():
            self.core_copy(t).wait_recv()
            self.acc[t % self.NA] = self.acc[t % self.NA] + self.inc[t % self.ND]
            pl.semaphore_signal(self.credit, inc=1, device_id=self.cube.devs[0], device_id_type=MESH)
            self.copy(0, t).start()

        for i in range(4):
            u = t - (i + 1) * self.LAG

            @pl.when((u >= 0) & (u < NU))
            def _(i=i, u=u):
                n = ROWS[i + 1]
                self.copy(i, u).wait()
                rows = pl.ds(aligned(self.cube.keep[i], n), n)
                value = self.acc[u % self.NA, rows, :] + self.recv[i][u % self.N]
                if i < 3:
                    self.acc[u % self.NA, rows, :] = value
                    self.copy(i + 1, u).start()
                else:
                    final(u, value)


class Gather:
    N = 8

    def __init__(self, cube, units, lag, block, ssem, rsem, first=None, local=None):
        self.cube, self.units, self.lag, self.block = cube, units, lag, block
        self.ssem, self.rsem, self.first, self.local = ssem, rsem, first, local

    @classmethod
    def scratch(cls):
        return [DMA((5, cls.N)), DMA((5, cls.N))]

    def copy(self, a, u):
        n = ROWS[4 - a]
        base = 0 if a == 4 else aligned(self.cube.keep[3 - a], n)
        here = self.block(u, pl.ds(base, n))
        src = self.first(u) if a == 0 and self.first is not None else here
        return remote(src, here, self.ssem.at[a, u % self.N], self.rsem.at[a, u % self.N], self.cube.devs[4 - a])

    def tick(self, t):
        for a in range(6):
            u = t - a * self.lag

            @pl.when((u >= 0) & (u < self.units))
            def _(a=a, u=u):
                if a > 0:
                    self.copy(a - 1, u).wait()
                if self.local is not None:
                    if a == 0:
                        self.local(u).start()
                    elif a == 1:
                        self.local(u).wait()
                if a < 5:
                    self.copy(a, u).start()


def small_scratch():
    return [pltpu.VMEM((6, 8, 128), f32), pltpu.VMEM((5, 8, 128), f32), DMA((5,)), DMA((5,))]


def small_step(cube, refs, i):
    mine, theirs, ssem, rsem = refs

    def copy(j):
        return remote(mine.at[j], theirs.at[j], ssem.at[j], rsem.at[j], cube.devs[j])

    if i > 0:
        copy(i - 1).wait()
        mine[i] = mine[i - 1] + theirs[i - 1]
    if i < 5:
        copy(i).start()


def fold(rows):
    out = jnp.zeros((8, 128), f32)
    for r in range(0, rows.shape[0], 8):
        for q in range(0, rows.shape[1], 128):
            out = out + rows[r : r + 8, q : q + 128]
    return out


def dot(a, b, ca=1, cb=0):
    return lax.dot_general(a, b, (((ca,), (cb,)), ((), ())), preferred_element_type=f32)


def forward_in(half, h_ref, cur, wa, u_ref, a_ref, rows):
    acc = dot(h_ref[cur, pl.ds(aligned(half * rows, 16), rows), :], wa)
    u = acc.astype(bf16)
    u_ref[half] = u
    a_ref[half] = gelu(u.astype(f32)).astype(bf16)


def forward_out(half, h_ref, cur, wb, transposed, a_ref, rows):
    rs = pl.ds(aligned(half * rows, 16), rows)
    acc = dot(a_ref[half], wb, 1, 1 if transposed else 0)
    h_ref[1 - cur, rs, :] = (h_ref[cur, rs, :].astype(f32) + acc).astype(bf16)


def forward_kernel(
    tokens, x_in, y_in, win, wout, hs, us, acts, d_out, a_out, b_out, shard_out,
    h, u, a, y, st_a, st_b, wa, wb, shard, turn, sx, sy, sa, sb, su, sact, sh, sao, sbo, sd, ss,
):
    rows = tokens // 2
    cube = Cube()
    row = cube.keep[3]
    col = cube.core * HALF

    def load_a(l):
        return pltpu.make_async_copy(win.at[l], st_a, sa)

    def load_b(l):
        return pltpu.make_async_copy(wout.at[l], st_b, sb)

    def save_u(l, r):
        return pltpu.make_async_copy(u.at[r], us.at[l, pl.ds(aligned(r * rows, 16), rows), :], su.at[r])

    def save_act(l, r):
        return pltpu.make_async_copy(a.at[r], acts.at[l, pl.ds(aligned(r * rows, 16), rows), :], sact.at[r])

    def save_h(l):
        return pltpu.make_async_copy(h.at[l % 2], hs.at[l], sh.at[l % 2])

    def save_a(l):
        return pltpu.make_async_copy(wa.at[l % 2], a_out.at[l], sao.at[l % 2])

    def save_b(l):
        return pltpu.make_async_copy(wb.at[l % 2], b_out.at[l], sbo.at[l % 2])

    copy_x = pltpu.make_async_copy(x_in, h.at[0], sx)
    copy_y = pltpu.make_async_copy(y_in, y, sy)
    load_a(0).start()
    copy_x.start()
    load_b(0).start()
    copy_y.start()
    copy_x.wait()
    save_h(0).start()

    def layer(l, carry):
        cur = l % 2
        k0 = (LAYERS - 1 - l) * 8

        @pl.when(l >= 2)
        def _():
            save_a(l - 2).wait()
            save_b(l - 2).wait()

        load_a(l).wait()

        def convert_a(i, carry):
            rs = pl.ds(aligned(i * 64, 64), 64)
            wa[cur, rs, :] = st_a[rs, :].astype(bf16)
            return carry

        lax.fori_loop(0, D // 64, convert_a, 0)
        for j in range(4):
            shard[k0 + 4 + j] = st_a[pl.ds(aligned(row, 32), 32), pl.ds(aligned(col + j * W, W), W)]
        save_a(l).start()

        @pl.when(l < LAYERS - 1)
        def _():
            load_a(l + 1).start()

        load_b(l).wait()

        def convert_b(i, carry):
            rs = pl.ds(aligned(i * 256, 256), 256)
            wb[cur, rs, :] = st_b[rs, :].astype(bf16)
            return carry

        lax.fori_loop(0, F // 256, convert_b, 0)
        for j in range(4):
            lanes = pl.ds(aligned((row // 128) * 128, 128), 128)
            turn[...] = st_b[pl.ds(aligned(col + j * W, W), W), lanes].T
            shard[k0 + j] = turn[pl.ds(aligned(row % 128, 32), 32), :]
        save_b(l).start()

        @pl.when(l < LAYERS - 1)
        def _():
            load_b(l + 1).start()

        def half_in(r, carry):
            @pl.when(l >= 1)
            def _():
                save_u(l - 1, r).wait()
                save_act(l - 1, r).wait()

            forward_in(r, h, cur, wa[cur], u, a, rows)
            save_u(l, r).start()
            save_act(l, r).start()
            return carry

        lax.fori_loop(0, 2, half_in, 0)

        @pl.when(l >= 1)
        def _():
            save_h(l - 1).wait()

        def half_out(r, carry):
            forward_out(r, h, cur, wb[cur], False, a, rows)
            return carry

        lax.fori_loop(0, 2, half_out, 0)

        @pl.when(l < LAYERS - 1)
        def _():
            save_h(l + 1).start()

        return carry

    lax.fori_loop(0, LAYERS, layer, 0)
    copy_y.wait()
    inv_count = 1.0 / (tokens * 32 * D)
    for r in range(2):
        rs = slice(r * rows, (r + 1) * rows)
        y[rs, :] = ((h[0, rs, :].astype(f32) - y[rs, :].astype(f32)) * inv_count).astype(bf16)
    save_d = pltpu.make_async_copy(y, d_out, sd)
    save_s = pltpu.make_async_copy(shard, shard_out, ss)
    save_d.start()
    save_s.start()
    for r in range(2):
        save_u(LAYERS - 1, r).wait()
        save_act(LAYERS - 1, r).wait()
        save_a(LAYERS - 2 + r).wait()
        save_b(LAYERS - 2 + r).wait()
    save_h(LAYERS - 1).wait()
    save_d.wait()
    save_s.wait()


def gather_forward_kernel(
    tokens, x_in, y_in, g_in, shard_in, norm_in, hs, us, acts, d_out, w_out, loss_out,
    h, u, a, y, wts, g, shard, norm, loss, sx, sy, sl, su, sact, sh, sw, sd, sloss, gsend, grecv,
):
    rows = tokens // 2
    radius = RHO_REL * math.sqrt(LAYERS * F + D)
    cube = Cube()
    row = cube.keep[3]
    col = cube.core * HALF
    lag = 1

    def save_u(l, r):
        return pltpu.make_async_copy(u.at[r], us.at[l, pl.ds(aligned(r * rows, 16), rows), :], su.at[r])

    def save_act(l, r):
        return pltpu.make_async_copy(a.at[r], acts.at[l, pl.ds(aligned(r * rows, 16), rows), :], sact.at[r])

    def save_h(l):
        return pltpu.make_async_copy(h.at[l % 2], hs.at[l], sh.at[l % 2])

    def save_w(m):
        return pltpu.make_async_copy(wts.at[m], w_out.at[m], sw.at[m])

    loads = [pltpu.make_async_copy(s, d, sl.at[i]) for i, (s, d) in enumerate(((norm_in, norm), (g_in, g), (shard_in, shard)))]
    copy_x = pltpu.make_async_copy(x_in, h.at[0], sx)
    copy_y = pltpu.make_async_copy(y_in, y, sy)
    for load in loads:
        load.start()
    copy_x.start()
    copy_y.start()
    cube.barrier()
    for load in loads:
        load.wait()
    total = jnp.sum(jnp.sum(norm[...], axis=0, keepdims=True), axis=1, keepdims=True)
    scale = radius / jnp.sqrt(total)

    def perturb(m, carry):
        k0 = (LAYERS - 1 - m // 2) * 8 + 4 - (m % 2) * 4
        for j in range(4):
            value = shard[k0 + j] + scale * g[k0 + j]
            wts[m, pl.ds(aligned(row, 32), 32), pl.ds(aligned(col + j * W, W), W)] = value.astype(bf16)
        return carry

    lax.fori_loop(0, 2 * LAYERS, perturb, 0)

    def block(unit, rs):
        return wts.at[unit // 2, rs, pl.ds(aligned(col + (unit % 2) * 512, 512), 512)]

    gather = Gather(cube, 4 * LAYERS, lag, block, gsend, grecv)
    lead = 5 * lag + 2

    def first(t, carry):
        gather.tick(t)
        return carry

    lax.fori_loop(0, lead, first, 0)
    copy_x.wait()
    save_h(0).start()

    def layer(l, carry):
        cur = l % 2
        save_w(2 * l).start()

        def half_in(r, carry):
            @pl.when(l >= 1)
            def _():
                save_u(l - 1, r).wait()
                save_act(l - 1, r).wait()

            forward_in(r, h, cur, wts[2 * l], u, a, rows)
            save_u(l, r).start()
            save_act(l, r).start()
            gather.tick(lead + 4 * l + r)
            return carry

        lax.fori_loop(0, 2, half_in, 0)
        save_w(2 * l + 1).start()

        @pl.when(l >= 1)
        def _():
            save_h(l - 1).wait()

        def half_out(r, carry):
            forward_out(r, h, cur, wts[2 * l + 1], True, a, rows)
            gather.tick(lead + 4 * l + 2 + r)
            return carry

        lax.fori_loop(0, 2, half_out, 0)

        @pl.when(l < LAYERS - 1)
        def _():
            save_h(l + 1).start()

        return carry

    lax.fori_loop(0, LAYERS, layer, 0)
    copy_y.wait()
    inv_count = 1.0 / (tokens * 32 * D)
    part = jnp.zeros((1, D), f32)
    for r in range(2):
        rs = slice(r * rows, (r + 1) * rows)
        diff = h[0, rs, :].astype(f32) - y[rs, :].astype(f32)
        y[rs, :] = (diff * inv_count).astype(bf16)
        part = part + jnp.sum(diff * diff, axis=0, keepdims=True)
    lanes = part[:, :128] + part[:, 128:256] + part[:, 256:384] + part[:, 384:]
    top = lax.broadcasted_iota(jnp.int32, (8, 128), 0) == 0
    loss[...] = jnp.where(top, jnp.broadcast_to(lanes, (8, 128)), 0.0)
    save_d = pltpu.make_async_copy(y, d_out, sd)
    save_loss = pltpu.make_async_copy(loss, loss_out, sloss)
    save_d.start()
    save_loss.start()
    for r in range(2):
        save_u(LAYERS - 1, r).wait()
        save_act(LAYERS - 1, r).wait()
    for m in range(2 * LAYERS):
        save_w(m).wait()
    save_h(LAYERS - 1).wait()
    save_d.wait()
    save_loss.wait()


def backward_compute(tokens, refs, cube, scatter, tick, load_a, load_b, transposed):
    (hs, us, acts, d_in, h, u, a, d, wa, wb, sh, su, sact, sd, sa, sb) = refs
    rows = tokens // 2
    own, other = cube.core * HALF, (1 - cube.core) * HALF

    def load(src, dst, sem):
        return pltpu.make_async_copy(src, dst, sem)

    def load_h(l):
        return load(hs.at[l], h, sh)

    def load_u(l):
        return load(us.at[l], u, su)

    def load_act(l):
        return load(acts.at[l], a, sact)

    load(d_in, d, sd).start()
    load_act(LAYERS - 1).start()
    load_u(LAYERS - 1).start()
    load_b(LAYERS - 1).start()
    load_h(LAYERS - 1).start()
    load_a(LAYERS - 1).start()
    cube.barrier()
    load(d_in, d, sd).wait()

    def produce(k, lhs, src, pair):
        scatter.before_write(k)
        scatter.before_write(k + 1)
        value = dot(lhs[...], src[:, pl.ds(aligned(other + pair * 512, 512), 512)], 0, 0)
        scatter.out[k % scatter.NSD] = value[:, :W]
        scatter.out[(k + 1) % scatter.NSD] = value[:, W:]
        scatter.push(k)
        scatter.push(k + 1)
        value = dot(lhs[...], src[:, pl.ds(aligned(own + pair * 512, 512), 512)], 0, 0)
        scatter.acc[k % scatter.NA] = value[:, :W]
        scatter.acc[(k + 1) % scatter.NA] = value[:, W:]

    def layer(i, carry):
        l = LAYERS - 1 - i
        more = i < LAYERS - 1
        load_act(l).wait()

        def out_pair(p, carry):
            produce(i * 8 + 2 * p, d, a, p)
            tick(i * 8 + p)
            return carry

        lax.fori_loop(0, 2, out_pair, 0)

        @pl.when(more)
        def _():
            load_act(l - 1).start()

        load_u(l).wait()
        load_b(l).wait()

        def slope_half(r, carry):
            rs = pl.ds(aligned(r * rows, 16), rows)
            for n in range(2):
                cs = slice(n * HALF, (n + 1) * HALF)
                if transposed:
                    da = dot(d[rs, :], wb[:, cs])
                else:
                    da = dot(d[rs, :], wb[cs, :], 1, 1)
                u[rs, cs] = (da * gelu_slope(u[rs, cs].astype(f32))).astype(bf16)
            tick(i * 8 + 2 + r)
            return carry

        lax.fori_loop(0, 2, slope_half, 0)

        @pl.when(more)
        def _():
            load_b(l - 1).start()

        load_h(l).wait()

        def in_pair(p, carry):
            produce(i * 8 + 4 + 2 * p, h, u, p)
            tick(i * 8 + 4 + p)
            return carry

        lax.fori_loop(0, 2, in_pair, 0)
        load_a(l).wait()

        @pl.when(more)
        def _():
            load_h(l - 1).start()

        def back_half(r, carry):
            @pl.when(more)
            def _():
                rs = pl.ds(aligned(r * rows, 16), rows)
                acc = dot(u[rs, :], wa[...], 1, 1)
                d[rs, :] = (d[rs, :].astype(f32) + acc).astype(bf16)

            tick(i * 8 + 6 + r)
            return carry

        lax.fori_loop(0, 2, back_half, 0)

        @pl.when(more)
        def _():
            load_a(l - 1).start()
            load_u(l - 1).start()

        return carry

    lax.fori_loop(0, LAYERS, layer, 0)


LEAD = 1


def backward_scatter_kernel(
    tokens, hs, us, acts, d_in, a_in, b_in, g_out, norm_out,
    h, u, a, d, wa, wb, sh, su, sact, sd, sa, sb, g, norm, sg, *refs,
):
    cube = Cube()
    scatter = ReduceScatter(cube, refs[:12])
    small = refs[12:]
    norm[...] = jnp.zeros_like(norm)

    def final(unit, value):
        g[unit] = value
        norm[...] += value * value

    def tick(t):
        scatter.tick(t - LEAD, final)

    backward_compute(
        tokens, (hs, us, acts, d_in, h, u, a, d, wa, wb, sh, su, sact, sd, sa, sb), cube, scatter, tick,
        lambda l: pltpu.make_async_copy(a_in.at[l], wa, sa), lambda l: pltpu.make_async_copy(b_in.at[l], wb, sb), False,
    )

    def rest(t, carry):
        tick(t)
        return carry

    lax.fori_loop(NU, scatter.TICKS + LEAD, rest, 0)
    save_g = pltpu.make_async_copy(g, g_out, sg.at[0])
    save_g.start()
    small[0][0] = fold(norm[...])
    for i in range(6):
        small_step(cube, small, i)
    save_n = pltpu.make_async_copy(small[0].at[5], norm_out, sg.at[1])
    save_n.start()
    scatter.finish()
    save_g.wait()
    save_n.wait()


def backward_update_kernel(
    tokens, hs, us, acts, d_in, w_in, shard_in, loss_in, new_out, loss_out,
    h, u, a, d, wa, wb, sh, su, sact, sd, sa, sb, shard, sg, slocal, gsend, grecv, *refs,
):
    cube = Cube()
    scatter = ReduceScatter(cube, refs[:12])
    small = refs[12:]
    row = cube.keep[3]
    lag = 2
    late = 4 * scatter.LAG + 1
    load_s = pltpu.make_async_copy(shard_in, shard, sg.at[0])
    load_l = pltpu.make_async_copy(loss_in, small[0].at[0], sg.at[1])
    load_s.start()
    load_l.start()

    def block(unit, rs):
        return new_out.at[unit, cube.core, rs, :]

    def local(unit):
        return pltpu.make_async_copy(
            shard.at[unit], block(unit, pl.ds(aligned(row, 32), 32)), slocal.at[unit % Gather.N]
        )

    gather = Gather(cube, NU, lag, block, gsend, grecv, lambda unit: shard.at[unit], local)

    def final(unit, value):
        shard[unit] = shard[unit] - LEARN_RATE * value

    def tick(t):
        for i in range(6):
            @pl.when(t == i)
            def _(i=i):
                if i == 0:
                    load_s.wait()
                    load_l.wait()
                small_step(cube, small, i)

        scatter.tick(t - LEAD, final)
        gather.tick(t - LEAD - late)

    backward_compute(
        tokens, (hs, us, acts, d_in, h, u, a, d, wa, wb, sh, su, sact, sd, sa, sb), cube, scatter, tick,
        lambda l: pltpu.make_async_copy(w_in.at[2 * l], wa, sa),
        lambda l: pltpu.make_async_copy(w_in.at[2 * l + 1], wb, sb), True,
    )

    def rest(t, carry):
        tick(t)
        return carry

    lax.fori_loop(NU, NU + late + LEAD + 5 * lag, rest, 0)
    save_l = pltpu.make_async_copy(small[0].at[5], loss_out, sg.at[1])
    save_l.start()
    scatter.finish()
    save_l.wait()


def place_kernel(out_part, in_part, new_in, new_out):
    new_in[...] = in_part[0, 0][None]
    new_out[...] = out_part[0, 0].T[None]


def solution(mesh):
    axes = tuple(mesh.axis_names)
    spec = P(axes, None, None)
    S = jax.ShapeDtypeStruct

    def step(images, targets, w_in, w_out):
        tokens = images.shape[0] * images.shape[1]
        rows = tokens // 2
        x = images.reshape(tokens, D)
        y = targets.reshape(tokens, D)
        saved = [S((LAYERS, tokens, D), bf16), S((LAYERS, tokens, F), bf16), S((LAYERS, tokens, F), bf16), S((tokens, D), bf16)]
        VM = pltpu.VMEM
        fwd_bufs = [VM((2, tokens, D), bf16), VM((2, rows, F), bf16), VM((2, rows, F), bf16), VM((tokens, D), bf16)]
        bwd_bufs = [VM((tokens, D), bf16), VM((tokens, F), bf16), VM((tokens, F), bf16), VM((tokens, D), bf16)]

        def call(kernel, outs, scratch, *args, collective=None):
            params = dict(vmem_limit_bytes=VMEM_LIMIT)
            if collective is not None:
                params.update(collective_id=collective, has_side_effects=True)
            return pl.pallas_call(
                lambda *refs: kernel(tokens, *refs),
                out_shape=outs,
                in_specs=[ANY] * len(args),
                out_specs=[ANY] * len(outs),
                scratch_shapes=scratch,
                compiler_params=pltpu.CompilerParams(**params),
                name=kernel.__name__,
            )(*args)

        hs, us, acts, d_top, a_bf, b_bf, shard = call(
            forward_kernel,
            saved + [S((LAYERS, D, F), bf16), S((LAYERS, F, D), bf16), S((NU, 32, W), f32)],
            fwd_bufs
            + [VM((D, F), f32), VM((F, D), f32), VM((2, D, F), bf16), VM((2, F, D), bf16), VM((NU, 32, W), f32), VM((128, W), f32)]
            + [DMA, DMA, DMA, DMA, DMA((2,)), DMA((2,)), DMA((2,)), DMA((2,)), DMA((2,)), DMA, DMA],
            x, y, w_in, w_out,
        )
        grads, norm = call(
            backward_scatter_kernel,
            [S((NU, 32, W), f32), S((8, 128), f32)],
            bwd_bufs
            + [VM((D, F), bf16), VM((F, D), bf16)]
            + [DMA] * 6
            + [VM((NU, 32, W), f32), VM((32, W), f32), DMA((2,))]
            + ReduceScatter.scratch()
            + small_scratch(),
            hs, us, acts, d_top, a_bf, b_bf,
            collective=1,
        )
        hs, us, acts, d_top, wts, loss = call(
            gather_forward_kernel,
            saved + [S((2 * LAYERS, D, F), bf16), S((8, 128), f32)],
            fwd_bufs
            + [VM((2 * LAYERS, D, F), bf16), VM((NU, 32, W), f32), VM((NU, 32, W), f32), VM((8, 128), f32), VM((8, 128), f32)]
            + [DMA, DMA, DMA((3,)), DMA((2,)), DMA((2,)), DMA((2,)), DMA((2 * LAYERS,)), DMA, DMA]
            + Gather.scratch(),
            x, y, grads, shard, norm,
            collective=2,
        )
        parts, loss = call(
            backward_update_kernel,
            [S((NU, 2, D, W), f32), S((8, 128), f32)],
            bwd_bufs
            + [VM((D, F), bf16), VM((D, F), bf16)]
            + [DMA] * 6
            + [VM((NU, 32, W), f32), DMA((2,)), DMA((Gather.N,))]
            + Gather.scratch()
            + ReduceScatter.scratch()
            + small_scratch(),
            hs, us, acts, d_top, wts, shard, loss,
            collective=3,
        )

        def part_spec(offset):
            return pl.BlockSpec((1, 1, D, W), lambda i: ((LAYERS - 1 - i // 8) * 8 + offset + i % 4, (i // 4) % 2, 0, 0))

        new_in, new_out = pl.pallas_call(
            place_kernel,
            out_shape=[S((LAYERS, D, F), f32), S((LAYERS, F, D), f32)],
            grid=(NU,),
            in_specs=[part_spec(0), part_spec(4)],
            out_specs=[pl.BlockSpec((1, D, W), lambda i: (i // 8, 0, i % 8)), pl.BlockSpec((1, W, D), lambda i: (i // 8, i % 8, 0))],
            name="place",
        )(parts, parts)
        inv_count = 1.0 / (tokens * math.prod(mesh.shape.values()) * D)
        return new_in, new_out, (0.5 * jnp.sum(loss)) * inv_count

    return jax.shard_map(step, mesh=mesh, in_specs=(spec, spec, P(), P()), out_specs=(P(), P(), P()), check_vma=False)
```

time: 1580 us -> 594 us (0.38)
  waiting for transfers between devices: 942 us -> 0 us
  Pallas kernels: 0 us -> 582 us
  matrix products: 429 us -> 0 us
  other arithmetic: 96.9 us -> 1.28 us
  blocking collectives: 40.5 us -> 0 us
  local copies, waits for them, and re-layouts: 41.2 us -> 6.57 us
  between operations: 22.8 us -> 2.45 us
    psum x2 -> x0, waiting for transfers between devices: 941 us -> none  [the longest x1 485 us: local_step(): grads_in, grads_out = lax.psum((grads_in, grads_out), mesh_axes)]
    pallas_call x0 -> x5, Pallas kernels: none -> 582 us  [the longest x4 548 us: call(): pl.pallas_call(lambda *refs: kernel(tokens, *refs), out_shape=outs, in_sp...]
    dot_general x44 -> x0, matrix products: 429 us -> none  [the longest x8 94.8 us: backward(): jnp.einsum('tf,td->fd', post_act, d_hidden, preferred_element_type=jnp.fl...]
    convert_element_type x4 -> x0, other arithmetic: 44.9 us -> none  [the longest x1 16.2 us: local_step(): (w_out[layer_idx] + step_scale * grads_out[layer_idx]).astype(jnp.bfloat16)]
    psum x1 -> x0, blocking collectives: 40.5 us -> none  [local_step(): lax.psum((grads2_in, grads2_out, loss_local), mesh_axes)]
    sub x2 -> x0, other arithmetic: 34.7 us -> none  [the longest x1 17.3 us: local_step(): new_in = w_in - LEARN_RATE * jnp.stack(grads2_in)]
    unnamed x115 -> x2, local copies, waits for them, and re-layouts: 35.6 us -> 3.84 us
    reduce_sum x4 -> x1, other arithmetic: 17.4 us -> 1.28 us  [step(): return (new_in, new_out, 0.5 * jnp.sum(loss) * inv_count)]
  transfers between devices with their start and end apart: 2 -> 0, of which waited for: 2 -> 0; matrix products, arithmetic and copies ran while one was open for 1% -> 0% of each run, Pallas kernels for 0% -> 0%
where the time goes in v1:
time: 594 us; the launch traced here: 593 us
  Pallas kernels  582 us (98%)
  local copies, waits for them, and re-layouts  6.57 us (1%)
    pallas_call x4, Pallas kernels, call(): pl.pallas_call(lambda *refs: kernel(tokens, *refs), out_shape=outs, in_sp...  548 us
    pallas_call x1, Pallas kernels, step(): pl.pallas_call(place_kernel, out_shape=[S((LAYERS, D, F), f32), S((LAYERS...  34.9 us

profile of v1, /device:TPU:0, one launch (start us, length us, event | category | flops | bytes accessed | tf_op | source)
XLA Modules:
  0.0 592.8 jit_solution(9060042555362838746)
XLA Ops:
  0.6 1.9 copy.9
  2.6 1.4 reshape.12.refs_0_
  3.9 1.9 copy.10
  5.8 1.4 reshape.13.refs_1_
  7.2 44.4 %forward_kernel.1 = (bf16[4,1568,512]{2,1,0:T(8,128)(2,1)}, bf16[4,1568,2048]{2,1,0:T(8,128)(2,1)}, bf16[4,1568,2048]{2,1,0:T(8,128)(2,1)}, bf16[1568,512]{1,0:T...) custom-call(bf16[1568,512]{1,0:T(8,128)(2,1)} %reshape.12.refs_0_, ...), custom_call_target="tpu_custom_call" | custom-call | tf_op jit(solution)/shard_map/forward_kernel/pallas_call | solution.py:729
  51.6 150.2 %backward_scatter_kernel.1 = (f32[32,32,256]{2,1,0:T(8,128)}, f32[8,128]{1,0:T(8,128)}) custom-call(bf16[4,1568,512]{2,1,0:T(8,128)(2,1)} %get-tuple-element.22.refs_0_, bf16[4,1568,2048]{2,1,0:T(8,128)(2,1)} %get-tuple-element.23.refs_1_, bf16[4,1568,2048]{2,1,0:T(8,128)(2,1)} %get-tuple-element.24.refs_2_, bf16[1568,512]{1,0:T(8,128)(2,1)} %get-tuple-element.25.refs_3_, ...), custom_call_target="tpu_custom_call" | custom-call | tf_op jit(solution)/shard_map/backward_scatter_kernel/pallas_call | solution.py:729
  201.8 93.5 %gather_forward_kernel.1 = (bf16[4,1568,512]{2,1,0:T(8,128)(2,1)}, bf16[4,1568,2048]{2,1,0:T(8,128)(2,1)}, bf16[4,1568,2048]{2,1,0:T(8,128)(2,1)}, bf16[1568,512...) custom-call(bf16[1568,512]{1,0:T(8,128)(2,1)} %reshape.12.refs_0_, ...), custom_call_target="tpu_custom_call" | custom-call | tf_op jit(solution)/shard_map/gather_forward_kernel/pallas_call | solution.py:729
  295.3 259.5 %backward_update_kernel.1 = (f32[32,2,512,256]{3,2,1,0:T(8,128)}, f32[8,128]{1,0:T(8,128)}) custom-call(bf16[4,1568,512]{2,1,0:T(8,128)(2,1)} %get-tuple-element.31.refs_0_, bf16[4,1568,2048]{2,1,0:T(8,128)(2,1)} %get-tuple-element.32.refs_1_, bf16[4,1568,2048]{2,1,0:T(8,128)(2,1)} %get-tuple-element.33.refs_2_, ...), custom_call_target="tpu_custom_call" | custom-call | tf_op jit(solution)/shard_map/backward_update_kernel/pallas_call | solution.py:729
  554.8 1.3 reduce_sum.9
  556.7 34.9 %place.1 = (f32[4,512,2048]{2,1,0:T(8,128)}, f32[4,2048,512]{2,1,0:T(8,128)}) custom-call(f32[32,2,512,256]{3,2,1,0:T(8,128)} %get-tuple-element.37.out_part.in_part, f32[32,2,512,256]{3,2,1,0:T(8,128)} %get-tuple-element.37.out_part.in_part), custom_call_target="tpu_custom_call" | custom-call | tf_op jit(solution)/shard_map/place/pallas_call | solution.py:786

commit v2 on v0

v2 whole, which is shorter than its diff:
```python
import math

import jax
import jax.numpy as jnp
from jax import lax
from jax.experimental import pallas as pl
from jax.experimental.pallas import tpu as pltpu
from jax.sharding import PartitionSpec as P

MESH = pl.DeviceIdType.MESH
f32 = jnp.float32
bf16 = jnp.bfloat16
RHO_REL = 0.1
LEARN_RATE = 8.0
SQRT_HALF = 0.7071067811865476
INV_SQRT_PI = 0.5641895835477563
LOG2_E = 1.4426950408889634
LAYERS, D, F = 4, 512, 2048
DEVICES = 32
HALF = F // 2
W = 256
NU = 32
ROWS = (512, 256, 128, 64, 32)
VMEM_LIMIT = 62 * 2**20

ANY = pl.BlockSpec(memory_space=pl.ANY)
DMA = pltpu.SemaphoreType.DMA


def aligned(value, multiple):
    return pl.multiple_of(value, multiple)


def gelu(x):
    return (0.5 * x) * (1.0 + lax.erf(x * SQRT_HALF))


def gelu_slope(x):
    z = x * SQRT_HALF
    return (0.5 + 0.5 * lax.erf(z)) + (z * INV_SQRT_PI) * jnp.exp2(z * z * (-LOG2_E))


def coords():
    z, y, dd = lax.axis_index("model"), lax.axis_index("sub"), lax.axis_index("data")
    return z, y, dd // 2, dd % 2


class Cube:
    def __init__(self):
        z, y, x, c = coords()
        fx, fy = 1 - 2 * x, 1 - 2 * y
        self.core = c
        self.devs = (
            (z, y, x * 2 + (1 - c)),
            (z, y + c * fy, (x + (1 - c) * fx) * 2 + c),
            (z + 1 - 2 * (z % 2), y, x * 2 + c),
            (z, y + (1 - c) * fy, (x + c * fx) * 2 + c),
            ((z + 2) % 4, y, x * 2 + c),
        )
        bits = (x * (1 - c) + y * c, z % 2, y * (1 - c) + x * c, z // 2)
        self.keep, self.give, base = [], [], 0
        for i in range(4):
            half = ROWS[i + 1]
            self.keep.append(base + bits[i] * half)
            self.give.append(base + (1 - bits[i]) * half)
            base = base + bits[i] * half

        self.me = (z * 2 + y) * 4 + x * 2 + c

    def other(self, i):
        n = lax.rem(self.me + i, DEVICES)
        return (n // 8, (n // 4) % 2, n % 4), n


def remote(src, dst, send_sem, recv_sem, dev):
    return pltpu.make_async_remote_copy(
        src_ref=src, dst_ref=dst, send_sem=send_sem, recv_sem=recv_sem, device_id=dev, device_id_type=MESH
    )


class ReduceScatter:
    NSD, ND, NA, N, LAG = 4, 8, 16, 8, 2
    TICKS = NU + 4 * LAG

    @classmethod
    def scratch(cls):
        n = cls.N
        return [
            pltpu.VMEM((cls.NSD, 512, W), f32),
            pltpu.VMEM((cls.NA, 512, W), f32),
            pltpu.VMEM((cls.ND, 512, W), f32),
            pltpu.VMEM((n, 256, W), f32),
            pltpu.VMEM((n, 128, W), f32),
            pltpu.VMEM((n, 64, W), f32),
            pltpu.VMEM((n, 32, W), f32),
            DMA((cls.NSD,)),
            DMA((cls.ND,)),
            DMA((4, n)),
            DMA((4, n)),
            pltpu.SemaphoreType.REGULAR,
        ]

    def __init__(self, cube, refs):
        self.cube = cube
        (self.out, self.acc, self.inc, r1, r2, r3, r4, self.dsend, self.drecv, self.ssem, self.rsem, self.credit) = refs
        self.recv = (r1, r2, r3, r4)

    def core_copy(self, k):
        return remote(
            self.out.at[k % self.NSD],
            self.inc.at[k % self.ND],
            self.dsend.at[k % self.NSD],
            self.drecv.at[k % self.ND],
            self.cube.devs[0],
        )

    def copy(self, i, k):
        n = ROWS[i + 1]
        return remote(
            self.acc.at[k % self.NA, pl.ds(aligned(self.cube.give[i], n), n), :],
            self.recv[i].at[k % self.N],
            self.ssem.at[i, k % self.N],
            self.rsem.at[i, k % self.N],
            self.cube.devs[i + 1],
        )

    def before_write(self, k):
        @pl.when(k >= self.NSD)
        def _():
            self.core_copy(k - self.NSD).wait_send()

    def push(self, k):
        @pl.when(k >= self.ND)
        def _():
            pl.semaphore_wait(self.credit, 1)

        self.core_copy(k).start()

    def finish(self):
        for k in range(NU - self.NSD, NU):
            self.core_copy(k).wait_send()
        pl.semaphore_wait(self.credit, self.ND)

    def begin(self, k):
        self.core_copy(k).wait_recv()
        self.acc[k % self.NA] = self.acc[k % self.NA] + self.inc[k % self.ND]
        pl.semaphore_signal(self.credit, inc=1, device_id=self.cube.devs[0], device_id_type=MESH)
        self.copy(0, k).start()

    def tick(self, t, final):
        for i in range(4):
            u = t - (i + 1) * self.LAG

            @pl.when((u >= 0) & (u < NU))
            def _(i=i, u=u):
                n = ROWS[i + 1]
                self.copy(i, u).wait()
                rows = pl.ds(aligned(self.cube.keep[i], n), n)
                value = self.acc[u % self.NA, rows, :] + self.recv[i][u % self.N]
                if i < 3:
                    self.acc[u % self.NA, rows, :] = value
                    self.copy(i + 1, u).start()
                else:
                    final(u, value)


class Gather:
    N = 8

    def __init__(self, cube, units, lag, block, ssem, rsem, first=None, local=None):
        self.cube, self.units, self.lag, self.block = cube, units, lag, block
        self.ssem, self.rsem, self.first, self.local = ssem, rsem, first, local

    @classmethod
    def scratch(cls):
        return [DMA((5, cls.N)), DMA((5, cls.N))]

    def copy(self, a, u):
        n = ROWS[4 - a]
        base = 0 if a == 4 else aligned(self.cube.keep[3 - a], n)
        here = self.block(u, pl.ds(base, n))
        src = self.first(u) if a == 0 and self.first is not None else here
        return remote(src, here, self.ssem.at[a, u % self.N], self.rsem.at[a, u % self.N], self.cube.devs[4 - a])

    def tick(self, t):
        for a in range(6):
            u = t - a * self.lag

            @pl.when((u >= 0) & (u < self.units))
            def _(a=a, u=u):
                if a > 0:
                    self.copy(a - 1, u).wait()
                if self.local is not None:
                    if a == 0:
                        self.local(u).start()
                    elif a == 1:
                        self.local(u).wait()
                if a < 5:
                    self.copy(a, u).start()


class Spread:
    def __init__(self, cube, refs):
        self.cube = cube
        self.tiles, self.mine, self.ssem, self.rsem = refs

    @staticmethod
    def scratch():
        return [pltpu.VMEM((DEVICES, 8, 128), f32), pltpu.VMEM((8, 128), f32), DMA((DEVICES,)), DMA((DEVICES,))]

    def copy(self, i, source):
        dev, _ = self.cube.other(i)
        return remote(self.mine, self.tiles.at[source], self.ssem.at[i], self.rsem.at[source], dev)

    def send(self, tile):
        self.mine[...] = tile
        self.tiles[self.cube.me] = tile

        def step(i, carry):
            self.copy(i, self.cube.me).start()
            return carry

        lax.fori_loop(1, DEVICES, step, 0)

    def total(self):
        def step(i, carry):
            _, source = self.cube.other(i)
            self.copy(i, source).wait_recv()
            self.copy(i, self.cube.me).wait_send()
            return carry

        lax.fori_loop(1, DEVICES, step, 0)
        out = self.tiles[0]
        for n in range(1, DEVICES):
            out = out + self.tiles[n]
        return out


def fold(rows):
    out = jnp.zeros((8, 128), f32)
    for r in range(0, rows.shape[0], 8):
        for q in range(0, rows.shape[1], 128):
            out = out + rows[r : r + 8, q : q + 128]
    return out


def dot(a, b, ca=1, cb=0):
    return lax.dot_general(a, b, (((ca,), (cb,)), ((), ())), preferred_element_type=f32)


def step_kernel(
    tokens, x_in, y_in, win, wout, parts, loss_out, hs, us, acts,
    h, u, a, d, wts, g, shard, turn, loss, norm,
    sx, sy, sa, sb, su, sact, sh, so, slocal, gsend, grecv, hsend, hrecv, *refs,
):
    rows = tokens // 2
    cube = Cube()
    scatter = ReduceScatter(cube, refs[:12])
    norm_sum = Spread(cube, refs[12:16])
    loss_sum = Spread(cube, refs[16:20])
    row = cube.keep[3]
    col = cube.core * HALF
    stage = scatter.acc
    inv_count = 1.0 / (tokens * DEVICES * D)
    barrier = pltpu.get_barrier_semaphore()

    def greet(i, carry):
        pl.semaphore_signal(barrier, inc=1, device_id=cube.other(i)[0], device_id_type=MESH)
        return carry

    def copy(src, dst, sem):
        return pltpu.make_async_copy(src, dst, sem)

    def part(r):
        return pl.ds(aligned(r * rows, 16), rows)

    def load_a(l, j):
        return copy(win.at[l, :, pl.ds(aligned(j * W, W), W)], stage.at[j], sa.at[j])

    def load_b(l, j):
        return copy(
            wout.at[l, pl.ds(aligned((j // 2) * 512, 512), 512), pl.ds(aligned((j % 2) * W, W), W)],
            stage.at[8 + j],
            sb.at[j],
        )

    def start_all(load, l):
        def step(j, carry):
            load(l, j).start()
            return carry

        lax.fori_loop(0, 8, step, 0)

    def wait_all(load, l):
        def step(j, carry):
            load(l, j).wait()
            return carry

        lax.fori_loop(0, 8, step, 0)

    def round_a(l, j):
        wts[2 * l, :, pl.ds(aligned(j * W, W), W)] = stage[j].astype(bf16)

    def round_b(l, j):
        block = stage[8 + j].T.astype(bf16)
        wts[2 * l + 1, pl.ds(aligned((j % 2) * W, W), W), pl.ds(aligned((j // 2) * 512, 512), 512)] = block

    def keep_a(l):
        for j in range(4):
            shard[(LAYERS - 1 - l) * 8 + 4 + j] = stage[cube.core * 4 + j, pl.ds(aligned(row, 32), 32), :]

    def keep_b(l):
        for j in range(4):
            slot = 8 + (cube.core * 2 + j // 2) * 2 + row // W
            lanes = pl.ds(aligned(((row % W) // 128) * 128, 128), 128)
            turn[...] = stage[slot, pl.ds((j % 2) * W, W), lanes].T
            shard[(LAYERS - 1 - l) * 8 + j] = turn[pl.ds(aligned(row % 128, 32), 32), :]

    def save_u(l, r):
        return copy(u.at[part(r), :], us.at[l, part(r), :], su.at[r])

    def save_act(l, r):
        return copy(a.at[part(r), :], acts.at[l, part(r), :], sact.at[r])

    def save_h(l):
        return copy(h.at[l % 2], hs.at[l], sh.at[l % 2])

    copy_x = copy(x_in, h.at[0], sx)
    copy_y = copy(y_in, d, sy)

    def forward(tick, before_in, before_out, beside_in, beside_out):
        def layer(l, carry):
            cur = l % 2
            before_in(l)

            def half_in(r, carry):
                @pl.when(l >= 1)
                def _():
                    save_u(l - 1, r).wait()
                    save_act(l - 1, r).wait()

                acc = dot(h[cur, part(r), :], wts[2 * l])
                pre = acc.astype(bf16)
                u[part(r), :] = pre
                a[part(r), :] = gelu(pre.astype(f32)).astype(bf16)
                beside_in(l, r)

                @pl.when(l < LAYERS - 1)
                def _():
                    save_u(l, r).start()
                    save_act(l, r).start()

                tick(4 * l + r)
                return carry

            lax.fori_loop(0, 2, half_in, 0)
            before_out(l)

            @pl.when(l >= 1)
            def _():
                save_h(l - 1).wait()

            def half_out(r, carry):
                acc = dot(a[part(r), :], wts[2 * l + 1], 1, 1)
                h[1 - cur, part(r), :] = (h[cur, part(r), :].astype(f32) + acc).astype(bf16)
                beside_out(l, r)
                tick(4 * l + 2 + r)
                return carry

            lax.fori_loop(0, 2, half_out, 0)

            @pl.when(l < LAYERS - 1)
            def _():
                save_h(l + 1).start()

            return carry

        lax.fori_loop(0, LAYERS, layer, 0)
        save_h(LAYERS - 1).wait()
        copy_y.wait()

    def backward(tick):
        own, away = cube.core * HALF, (1 - cube.core) * HALF

        def load_h(l):
            return copy(hs.at[l], h.at[1], sh.at[1])

        def load_u(l):
            return copy(us.at[l], u, su.at[0])

        def load_act(l):
            return copy(acts.at[l], a, sact.at[0])

        def produce(k, lhs, src, pair):
            scatter.before_write(k)
            scatter.before_write(k + 1)
            value = dot(lhs[...], src[:, pl.ds(aligned(away + pair * 512, 512), 512)], 0, 0)
            scatter.out[k % scatter.NSD] = value[:, :W]
            scatter.out[(k + 1) % scatter.NSD] = value[:, W:]
            scatter.push(k)
            scatter.push(k + 1)
            value = dot(lhs[...], src[:, pl.ds(aligned(own + pair * 512, 512), 512)], 0, 0)
            scatter.acc[k % scatter.NA] = value[:, :W]
            scatter.acc[(k + 1) % scatter.NA] = value[:, W:]

        def begin_pair(k, p):
            @pl.when(p == 1)
            def _():
                scatter.begin(k - 1)

            scatter.begin(k)

        def begin_last(k, r):
            @pl.when(r == 0)
            def _():
                scatter.begin(k)

        def layer(i, carry):
            l = LAYERS - 1 - i
            more = i < LAYERS - 1

            @pl.when(i > 0)
            def _():
                load_act(l).wait()

            def out_pair(p, carry):
                produce(i * 8 + 2 * p, d, a, p)
                begin_pair(i * 8 + 2 * p, p)
                tick(i * 8 + p)
                return carry

            lax.fori_loop(0, 2, out_pair, 0)

            @pl.when(more)
            def _():
                load_act(l - 1).start()

            @pl.when(i > 0)
            def _():
                load_u(l).wait()

            def slope_half(r, carry):
                for n in range(2):
                    cs = slice(n * HALF, (n + 1) * HALF)
                    da = dot(d[part(r), :], wts[2 * l + 1, :, cs])
                    u[part(r), cs] = (da * gelu_slope(u[part(r), cs].astype(f32))).astype(bf16)
                begin_last(i * 8 + 3, r)
                tick(i * 8 + 2 + r)
                return carry

            lax.fori_loop(0, 2, slope_half, 0)

            @pl.when(i > 0)
            def _():
                load_h(l).wait()

            def in_pair(p, carry):
                produce(i * 8 + 4 + 2 * p, h.at[1], u, p)
                begin_pair(i * 8 + 4 + 2 * p, p)
                tick(i * 8 + 4 + p)
                return carry

            lax.fori_loop(0, 2, in_pair, 0)

            @pl.when(more)
            def _():
                load_h(l - 1).start()

            def back_half(r, carry):
                @pl.when(more)
                def _():
                    acc = dot(u[part(r), :], wts[2 * l], 1, 1)
                    d[part(r), :] = (d[part(r), :].astype(f32) + acc).astype(bf16)

                begin_last(i * 8 + 7, r)
                tick(i * 8 + 6 + r)
                return carry

            lax.fori_loop(0, 2, back_half, 0)

            @pl.when(more)
            def _():
                load_u(l - 1).start()

            return carry

        lax.fori_loop(0, LAYERS, layer, 0)

    def nothing(*_):
        pass

    copy_x.start()
    start_all(load_a, 0)
    start_all(load_b, 0)
    copy_y.start()
    lax.fori_loop(1, DEVICES, greet, 0)
    copy_x.wait()
    save_h(0).start()
    wait_all(load_a, 0)

    def round_first(j, carry):
        round_a(0, j)
        return carry

    lax.fori_loop(0, 8, round_first, 0)

    def before_in_1(l):
        @pl.when(l == 0)
        def _():
            keep_a(0)

        wait_all(load_b, l)
        keep_b(l)

        @pl.when(l < LAYERS - 1)
        def _():
            start_all(load_a, l + 1)

    def beside_in_1(l, r):
        for j in range(4):
            round_b(l, r * 4 + j)

    def before_out_1(l):
        @pl.when(l < LAYERS - 1)
        def _():
            start_all(load_b, l + 1)
            wait_all(load_a, l + 1)
            keep_a(l + 1)

    def beside_out_1(l, r):
        for j in range(4):
            round_a(jnp.minimum(l + 1, LAYERS - 1), r * 4 + j)

    forward(nothing, before_in_1, before_out_1, beside_in_1, beside_out_1)
    for r in range(2):
        diff = h[0, part(r), :].astype(f32) - d[part(r), :].astype(f32)
        d[part(r), :] = (diff * inv_count).astype(bf16)
    pl.semaphore_wait(barrier, DEVICES - 1)

    norm[...] = jnp.zeros_like(norm)

    def final_1(unit, value):
        g[unit] = value
        norm[...] += value * value

    def tick_1(t):
        scatter.tick(t, final_1)

    backward(tick_1)

    def rest_1(t, carry):
        tick_1(t)
        return carry

    copy_x.start()
    lax.fori_loop(NU, scatter.TICKS, rest_1, 0)
    norm_sum.send(fold(norm[...]))
    copy_y.start()
    scatter.finish()
    total = norm_sum.total()
    total = jnp.sum(jnp.sum(total, axis=0, keepdims=True), axis=1, keepdims=True)
    scale = (RHO_REL * math.sqrt(LAYERS * F + D)) / jnp.sqrt(total)

    def perturb(m, carry):
        k0 = (LAYERS - 1 - m // 2) * 8 + 4 - (m % 2) * 4
        for j in range(4):
            value = shard[k0 + j] + scale * g[k0 + j]
            wts[m, pl.ds(aligned(row, 32), 32), pl.ds(aligned(col + j * W, W), W)] = value.astype(bf16)
        return carry

    lax.fori_loop(0, 2 * LAYERS, perturb, 0)

    def weight_block(unit, rs):
        return wts.at[unit // 2, rs, pl.ds(aligned(col + (unit % 2) * 512, 512), 512)]

    weights = Gather(cube, 4 * LAYERS, 2, weight_block, gsend, grecv)
    lead = 5 * weights.lag + 2

    def first(t, carry):
        weights.tick(t)
        return carry

    lax.fori_loop(0, lead, first, 0)
    copy_x.wait()
    save_h(0).start()
    forward(lambda t: weights.tick(lead + t), nothing, nothing, nothing, nothing)
    squares = jnp.zeros((1, D), f32)
    for r in range(2):
        diff = h[0, part(r), :].astype(f32) - d[part(r), :].astype(f32)
        d[part(r), :] = (diff * inv_count).astype(bf16)
        squares = squares + jnp.sum(diff * diff, axis=0, keepdims=True)
    lanes = squares[:, :128] + squares[:, 128:256] + squares[:, 256:384] + squares[:, 384:]
    top = lax.broadcasted_iota(jnp.int32, (8, 128), 0) == 0
    loss_sum.send(jnp.where(top, jnp.broadcast_to(lanes, (8, 128)), 0.0))

    late = 4 * scatter.LAG + 1

    def new_block(unit, rs):
        return parts.at[unit, cube.core, rs, :]

    def local(unit):
        return copy(shard.at[unit], new_block(unit, pl.ds(aligned(row, 32), 32)), slocal.at[unit % Gather.N])

    updates = Gather(cube, NU, 2, new_block, hsend, hrecv, lambda unit: shard.at[unit], local)

    def final_2(unit, value):
        shard[unit] = shard[unit] - LEARN_RATE * value

    def tick_2(t):
        scatter.tick(t, final_2)
        updates.tick(t - late)

    backward(tick_2)

    def rest_2(t, carry):
        tick_2(t)
        return carry

    lax.fori_loop(NU, NU + late + 5 * updates.lag, rest_2, 0)
    scatter.finish()
    loss[...] = loss_sum.total()
    save_loss = copy(loss, loss_out, so)
    save_loss.start()
    save_loss.wait()


def place_kernel(tokens, parts, new_in, new_out, straight, before, after, s_load, s_store, t_load, t_store):
    slots, ahead = straight.shape[0], 4

    def where(n):
        return n // 8, (n // 4) % 2, n % 4

    def load_in(n):
        l, c, j = where(n)
        return pltpu.make_async_copy(parts.at[(LAYERS - 1 - l) * 8 + 4 + j, c], straight.at[n % slots], s_load.at[n % slots])

    def store_in(n):
        l, c, j = where(n)
        cols = pl.ds(aligned(c * HALF + j * W, W), W)
        return pltpu.make_async_copy(straight.at[n % slots], new_in.at[l, :, cols], s_store.at[n % slots])

    def load_out(n):
        l, c, j = where(n)
        return pltpu.make_async_copy(parts.at[(LAYERS - 1 - l) * 8 + j, c], before.at[n % slots], t_load.at[n % slots])

    def store_out(n):
        l, c, j = where(n)
        rows = pl.ds(aligned(c * HALF + j * W, W), W)
        return pltpu.make_async_copy(after.at[n % slots], new_out.at[l, rows, :], t_store.at[n % slots])

    for n in range(ahead):
        load_in(n).start()
        load_out(n).start()

    def step(n, carry):
        load_in(n).wait()
        store_in(n).start()

        @pl.when(n >= slots)
        def _():
            store_out(n - slots).wait()

        load_out(n).wait()
        after[n % slots] = before[n % slots].T
        store_out(n).start()

        @pl.when(n + ahead < NU)
        def _():
            @pl.when(n + ahead >= slots)
            def _():
                store_in(n + ahead - slots).wait()

            load_in(n + ahead).start()
            load_out(n + ahead).start()

        return carry

    lax.fori_loop(0, NU, step, 0)
    for n in range(NU - slots, NU):
        store_in(n).wait()
        store_out(n).wait()


def solution(mesh):
    axes = tuple(mesh.axis_names)
    spec = P(axes, None, None)
    S = jax.ShapeDtypeStruct
    VM = pltpu.VMEM

    def step(images, targets, w_in, w_out):
        tokens = images.shape[0] * images.shape[1]
        x = jnp.swapaxes(images, 0, 1).reshape(tokens, D)
        y = jnp.swapaxes(targets, 0, 1).reshape(tokens, D)

        def call(kernel, outs, scratch, *args, collective=None):
            params = dict(vmem_limit_bytes=VMEM_LIMIT)
            if collective is not None:
                params.update(collective_id=collective, has_side_effects=True)
            return pl.pallas_call(
                lambda *refs: kernel(tokens, *refs),
                out_shape=outs,
                in_specs=[ANY] * len(args),
                out_specs=[ANY] * len(outs),
                scratch_shapes=scratch,
                compiler_params=pltpu.CompilerParams(**params),
                name=kernel.__name__,
            )(*args)

        parts, loss, _, _, _ = call(
            step_kernel,
            [S((NU, 2, D, W), f32), S((8, 128), f32), S((LAYERS, tokens, D), bf16)]
            + [S((LAYERS - 1, tokens, F), bf16)] * 2,
            [VM((2, tokens, D), bf16), VM((tokens, F), bf16), VM((tokens, F), bf16), VM((tokens, D), bf16)]
            + [VM((2 * LAYERS, D, F), bf16), VM((NU, 32, W), f32), VM((NU, 32, W), f32), VM((128, W), f32)]
            + [VM((8, 128), f32), VM((32, W), f32)]
            + [DMA, DMA, DMA((8,)), DMA((8,)), DMA((2,)), DMA((2,)), DMA((2,)), DMA, DMA((Gather.N,))]
            + Gather.scratch()
            + Gather.scratch()
            + ReduceScatter.scratch()
            + Spread.scratch()
            + Spread.scratch(),
            x, y, w_in, w_out,
            collective=1,
        )
        new_in, new_out = call(
            place_kernel,
            [S((LAYERS, D, F), f32), S((LAYERS, F, D), f32)],
            [VM((8, D, W), f32), VM((8, D, W), f32), VM((8, W, D), f32)] + [DMA((8,))] * 4,
            parts,
        )
        return new_in, new_out, (0.5 * jnp.sum(loss)) * (1.0 / (tokens * DEVICES * D))

    return jax.shard_map(step, mesh=mesh, in_specs=(spec, spec, P(), P()), out_specs=(P(), P(), P()), check_vma=False)
```

time: 1580 us -> 541 us (0.34)
  waiting for transfers between devices: 942 us -> 0 us
  Pallas kernels: 0 us -> 537 us
  matrix products: 429 us -> 0 us
  other arithmetic: 96.9 us -> 1.29 us
  local copies, waits for them, and re-layouts: 41.2 us -> 0 us
  blocking collectives: 40.5 us -> 0 us
  between operations: 22.8 us -> 2.43 us
    psum x2 -> x0, waiting for transfers between devices: 941 us -> none  [the longest x1 485 us: local_step(): grads_in, grads_out = lax.psum((grads_in, grads_out), mesh_axes)]
    pallas_call x0 -> x2, Pallas kernels: none -> 537 us  [call(): pl.pallas_call(lambda *refs: kernel(tokens, *refs), out_shape=outs, in_sp...]
    dot_general x44 -> x0, matrix products: 429 us -> none  [the longest x8 94.8 us: backward(): jnp.einsum('tf,td->fd', post_act, d_hidden, preferred_element_type=jnp.fl...]
    convert_element_type x4 -> x0, other arithmetic: 44.9 us -> none  [the longest x1 16.2 us: local_step(): (w_out[layer_idx] + step_scale * grads_out[layer_idx]).astype(jnp.bfloat16)]
    psum x1 -> x0, blocking collectives: 40.5 us -> none  [local_step(): lax.psum((grads2_in, grads2_out, loss_local), mesh_axes)]
    unnamed x115 -> x0, local copies, waits for them, and re-layouts: 35.6 us -> none
    sub x2 -> x0, other arithmetic: 34.7 us -> none  [the longest x1 17.3 us: local_step(): new_in = w_in - LEARN_RATE * jnp.stack(grads2_in)]
    reduce_sum x4 -> x1, other arithmetic: 17.4 us -> 1.29 us  [step(): jnp.sum(loss)]
  transfers between devices with their start and end apart: 2 -> 0, of which waited for: 2 -> 0; matrix products, arithmetic and copies ran while one was open for 1% -> 0% of each run, Pallas kernels for 0% -> 0%
where the time goes in v2:
time: 541 us
  Pallas kernels  537 us (99%)
    pallas_call x2, Pallas kernels, call(): pl.pallas_call(lambda *refs: kernel(tokens, *refs), out_shape=outs, in_sp...  537 us

profile of v2, /device:TPU:0, one launch (start us, length us, event | category | flops | bytes accessed | tf_op | source)
XLA Modules:
  0.0 540.8 jit_solution(6476077538256576333)
XLA Ops:
  0.6 514.4 %step_kernel.1 = (f32[32,2,512,256]{3,2,1,0:T(8,128)}, f32[8,128]{1,0:T(8,128)}, bf16[4,1568,512]{2,1,0:T(8,128)(2,1)}, bf16[3,1568,2048]{2,1,0:T(8,128)(2,1)}, bf16[3,1568,2048]{2,1,0:T(8,128)(2,1)}) custom-call(bf16[1568,512]{1,0:T(8,128)(2,1)} %bitcast.6, bf16[1568,512]{1,0:T(8,128)(2,1)} %bitcast.7, f32[4,512,2048]{2,1,0:T(8,128)} %refs_2_.1, ...), custom_call_target="tpu_custom_call" | custom-call | tf_op jit(solution)/shard_map/step_kernel/pallas_call | solution.py:699
  515.1 1.3 reduce_sum.9
  517.0 22.7 %place_kernel.1 = (f32[4,512,2048]{2,1,0:T(8,128)}, f32[4,2048,512]{2,1,0:T(8,128)}) custom-call(f32[32,2,512,256]{3,2,1,0:T(8,128)} %get-tuple-element.7.refs_0_), custom_call_target="tpu_custom_call" | custom-call | tf_op jit(solution)/shard_map/place_kernel/pallas_call | solution.py:699

commit v3 on v2

--- a/solution.py
+++ b/solution.py
@@ -31,13 +31,14 @@
     return pl.multiple_of(value, multiple)
 
 
-def gelu(x):
-    return (0.5 * x) * (1.0 + lax.erf(x * SQRT_HALF))
-
-
-def gelu_slope(x):
+def gelu(u):
+    half = (u * bf16(0.5)).astype(f32)
+    return half * (1.0 + lax.erf(half * (2.0 * SQRT_HALF)))
+
+
+def gelu_slope_twice(x):
     z = x * SQRT_HALF
-    return (0.5 + 0.5 * lax.erf(z)) + (z * INV_SQRT_PI) * jnp.exp2(z * z * (-LOG2_E))
+    return (1.0 + lax.erf(z)) + (z * (2.0 * INV_SQRT_PI)) * jnp.exp2(z * z * (-LOG2_E))
 
 
 def coords():
@@ -167,8 +168,8 @@
 class Gather:
     N = 8
 
-    def __init__(self, cube, units, lag, block, ssem, rsem, first=None, local=None):
-        self.cube, self.units, self.lag, self.block = cube, units, lag, block
+    def __init__(self, cube, units, begins, block, ssem, rsem, first=None, local=None):
+        self.cube, self.units, self.begins, self.block = cube, units, begins, block
         self.ssem, self.rsem, self.first, self.local = ssem, rsem, first, local
 
     @classmethod
@@ -184,7 +185,7 @@
 
     def tick(self, t):
         for a in range(6):
-            u = t - a * self.lag
+            u = t - self.begins[a]
 
             @pl.when((u >= 0) & (u < self.units))
             def _(a=a, u=u):
@@ -285,18 +286,12 @@
         )
 
     def start_all(load, l):
-        def step(j, carry):
+        for j in range(8):
             load(l, j).start()
-            return carry
-
-        lax.fori_loop(0, 8, step, 0)
 
     def wait_all(load, l):
-        def step(j, carry):
+        for j in range(8):
             load(l, j).wait()
-            return carry
-
-        lax.fori_loop(0, 8, step, 0)
 
     def round_a(l, j):
         wts[2 * l, :, pl.ds(aligned(j * W, W), W)] = stage[j].astype(bf16)
@@ -305,16 +300,14 @@
         block = stage[8 + j].T.astype(bf16)
         wts[2 * l + 1, pl.ds(aligned((j % 2) * W, W), W), pl.ds(aligned((j // 2) * 512, 512), 512)] = block
 
-    def keep_a(l):
-        for j in range(4):
-            shard[(LAYERS - 1 - l) * 8 + 4 + j] = stage[cube.core * 4 + j, pl.ds(aligned(row, 32), 32), :]
-
-    def keep_b(l):
-        for j in range(4):
-            slot = 8 + (cube.core * 2 + j // 2) * 2 + row // W
-            lanes = pl.ds(aligned(((row % W) // 128) * 128, 128), 128)
-            turn[...] = stage[slot, pl.ds((j % 2) * W, W), lanes].T
-            shard[(LAYERS - 1 - l) * 8 + j] = turn[pl.ds(aligned(row % 128, 32), 32), :]
+    def keep_a(l, j):
+        shard[(LAYERS - 1 - l) * 8 + 4 + j] = stage[cube.core * 4 + j, pl.ds(aligned(row, 32), 32), :]
+
+    def keep_b(l, j):
+        slot = 8 + (cube.core * 2 + j // 2) * 2 + row // W
+        lanes = pl.ds(aligned(((row % W) // 128) * 128, 128), 128)
+        turn[j] = stage[slot, pl.ds(aligned((j % 2) * W, W), W), lanes].T
+        shard[(LAYERS - 1 - l) * 8 + j] = turn[j, pl.ds(aligned(row % 128, 32), 32), :]
 
     def save_u(l, r):
         return copy(u.at[part(r), :], us.at[l, part(r), :], su.at[r])
@@ -328,46 +321,62 @@
     copy_x = copy(x_in, h.at[0], sx)
     copy_y = copy(y_in, d, sy)
 
-    def forward(tick, before_in, before_out, beside_in, beside_out):
+    def forward(tick, before_in, before_out, beside_in, beside_out, whole):
         def layer(l, carry):
             cur = l % 2
-            before_in(l)
-
-            def half_in(r, carry):
+
+            def wait_saves(r):
                 @pl.when(l >= 1)
                 def _():
                     save_u(l - 1, r).wait()
                     save_act(l - 1, r).wait()
 
-                acc = dot(h[cur, part(r), :], wts[2 * l])
-                pre = acc.astype(bf16)
-                u[part(r), :] = pre
-                a[part(r), :] = gelu(pre.astype(f32)).astype(bf16)
-                beside_in(l, r)
-
+            def start_saves(r):
                 @pl.when(l < LAYERS - 1)
                 def _():
                     save_u(l, r).start()
                     save_act(l, r).start()
 
-                tick(4 * l + r)
-                return carry
-
-            lax.fori_loop(0, 2, half_in, 0)
-            before_out(l)
-
-            @pl.when(l >= 1)
-            def _():
-                save_h(l - 1).wait()
-
-            def half_out(r, carry):
+            def rows_in(r):
+                u[part(r), :] = dot(h[cur, part(r), :], wts[2 * l]).astype(bf16)
+                a[part(r), :] = gelu(u[part(r), :]).astype(bf16)
+                beside_in(l, r)
+
+            def rows_out(r):
                 acc = dot(a[part(r), :], wts[2 * l + 1], 1, 1)
                 h[1 - cur, part(r), :] = (h[cur, part(r), :].astype(f32) + acc).astype(bf16)
                 beside_out(l, r)
+
+            def half_in(r, carry):
+                wait_saves(r)
+                rows_in(r)
+                start_saves(r)
+                tick(4 * l + r)
+                return carry
+
+            def half_out(r, carry):
+                rows_out(r)
                 tick(4 * l + 2 + r)
                 return carry
 
-            lax.fori_loop(0, 2, half_out, 0)
+            before_in(l)
+            if whole:
+                for step in (wait_saves, rows_in, start_saves):
+                    for r in range(2):
+                        step(r)
+            else:
+                lax.fori_loop(0, 2, half_in, 0)
+            before_out(l)
+
+            @pl.when(l >= 1)
+            def _():
+                save_h(l - 1).wait()
+
+            if whole:
+                for r in range(2):
+                    rows_out(r)
+            else:
+                lax.fori_loop(0, 2, half_out, 0)
 
             @pl.when(l < LAYERS - 1)
             def _():
@@ -440,10 +449,11 @@
                 load_u(l).wait()
 
             def slope_half(r, carry):
+                half = d[part(r), :] * bf16(0.5)
                 for n in range(2):
                     cs = slice(n * HALF, (n + 1) * HALF)
-                    da = dot(d[part(r), :], wts[2 * l + 1, :, cs])
-                    u[part(r), cs] = (da * gelu_slope(u[part(r), cs].astype(f32))).astype(bf16)
+                    da = dot(half, wts[2 * l + 1, :, cs])
+                    u[part(r), cs] = (da * gelu_slope_twice(u[part(r), cs].astype(f32))).astype(bf16)
                 begin_last(i * 8 + 3, r)
                 tick(i * 8 + 2 + r)
                 return carry
@@ -496,21 +506,18 @@
     lax.fori_loop(1, DEVICES, greet, 0)
     copy_x.wait()
     save_h(0).start()
-    wait_all(load_a, 0)
 
     def round_first(j, carry):
+        load_a(0, j).wait()
         round_a(0, j)
         return carry
 
     lax.fori_loop(0, 8, round_first, 0)
+    for j in range(4):
+        keep_a(0, j)
 
     def before_in_1(l):
-        @pl.when(l == 0)
-        def _():
-            keep_a(0)
-
         wait_all(load_b, l)
-        keep_b(l)
 
         @pl.when(l < LAYERS - 1)
         def _():
@@ -519,19 +526,23 @@
     def beside_in_1(l, r):
         for j in range(4):
             round_b(l, r * 4 + j)
+        for j in range(2):
+            keep_b(l, r * 2 + j)
 
     def before_out_1(l):
         @pl.when(l < LAYERS - 1)
         def _():
             start_all(load_b, l + 1)
             wait_all(load_a, l + 1)
-            keep_a(l + 1)
 
     def beside_out_1(l, r):
+        following = jnp.minimum(l + 1, LAYERS - 1)
         for j in range(4):
-            round_a(jnp.minimum(l + 1, LAYERS - 1), r * 4 + j)
-
-    forward(nothing, before_in_1, before_out_1, beside_in_1, beside_out_1)
+            round_a(following, r * 4 + j)
+        for j in range(2):
+            keep_a(following, r * 2 + j)
+
+    forward(nothing, before_in_1, before_out_1, beside_in_1, beside_out_1, False)
     for r in range(2):
         diff = h[0, part(r), :].astype(f32) - d[part(r), :].astype(f32)
         d[part(r), :] = (diff * inv_count).astype(bf16)
@@ -573,8 +584,8 @@
     def weight_block(unit, rs):
         return wts.at[unit // 2, rs, pl.ds(aligned(col + (unit % 2) * 512, 512), 512)]
 
-    weights = Gather(cube, 4 * LAYERS, 2, weight_block, gsend, grecv)
-    lead = 5 * weights.lag + 2
+    weights = Gather(cube, 4 * LAYERS, (0, 2, 4, 6, 8, 9), weight_block, gsend, grecv)
+    lead = weights.begins[5] + 2
 
     def first(t, carry):
         weights.tick(t)
@@ -583,7 +594,7 @@
     lax.fori_loop(0, lead, first, 0)
     copy_x.wait()
     save_h(0).start()
-    forward(lambda t: weights.tick(lead + t), nothing, nothing, nothing, nothing)
+    forward(lambda t: weights.tick(lead + t), nothing, nothing, nothing, nothing, False)
     squares = jnp.zeros((1, D), f32)
     for r in range(2):
         diff = h[0, part(r), :].astype(f32) - d[part(r), :].astype(f32)
@@ -601,7 +612,7 @@
     def local(unit):
         return copy(shard.at[unit], new_block(unit, pl.ds(aligned(row, 32), 32)), slocal.at[unit % Gather.N])
 
-    updates = Gather(cube, NU, 2, new_block, hsend, hrecv, lambda unit: shard.at[unit], local)
+    updates = Gather(cube, NU, (0, 2, 4, 6, 8, 10), new_block, hsend, hrecv, lambda unit: shard.at[unit], local)
 
     def final_2(unit, value):
         shard[unit] = shard[unit] - LEARN_RATE * value
@@ -616,7 +627,7 @@
         tick_2(t)
         return carry
 
-    lax.fori_loop(NU, NU + late + 5 * updates.lag, rest_2, 0)
+    lax.fori_loop(NU, NU + late + updates.begins[5], rest_2, 0)
     scatter.finish()
     loss[...] = loss_sum.total()
     save_loss = copy(loss, loss_out, so)
@@ -624,7 +635,7 @@
     save_loss.wait()
 
 
-def place_kernel(tokens, parts, new_in, new_out, straight, before, after, s_load, s_store, t_load, t_store):
+def place_kernel(tokens, parts, loss_in, new_in, new_out, loss_out, straight, before, after, loss, s_load, s_store, t_load, t_store, sl):
     slots, ahead = straight.shape[0], 4
 
     def where(n):
@@ -648,9 +659,13 @@
         rows = pl.ds(aligned(c * HALF + j * W, W), W)
         return pltpu.make_async_copy(after.at[n % slots], new_out.at[l, rows, :], t_store.at[n % slots])
 
+    load_loss = pltpu.make_async_copy(loss_in, loss, sl)
+    load_loss.start()
     for n in range(ahead):
         load_in(n).start()
         load_out(n).start()
+    load_loss.wait()
+    loss_out[0, 0] = (0.5 * jnp.sum(loss[...])) * (1.0 / (tokens * DEVICES * D))
 
     def step(n, carry):
         load_in(n).wait()
@@ -692,7 +707,7 @@
         x = jnp.swapaxes(images, 0, 1).reshape(tokens, D)
         y = jnp.swapaxes(targets, 0, 1).reshape(tokens, D)
 
-        def call(kernel, outs, scratch, *args, collective=None):
+        def call(kernel, outs, scratch, *args, collective=None, out_specs=None):
             params = dict(vmem_limit_bytes=VMEM_LIMIT)
             if collective is not None:
                 params.update(collective_id=collective, has_side_effects=True)
@@ -700,7 +715,7 @@
                 lambda *refs: kernel(tokens, *refs),
                 out_shape=outs,
                 in_specs=[ANY] * len(args),
-                out_specs=[ANY] * len(outs),
+                out_specs=out_specs or [ANY] * len(outs),
                 scratch_shapes=scratch,
                 compiler_params=pltpu.CompilerParams(**params),
                 name=kernel.__name__,
@@ -711,7 +726,7 @@
             [S((NU, 2, D, W), f32), S((8, 128), f32), S((LAYERS, tokens, D), bf16)]
             + [S((LAYERS - 1, tokens, F), bf16)] * 2,
             [VM((2, tokens, D), bf16), VM((tokens, F), bf16), VM((tokens, F), bf16), VM((tokens, D), bf16)]
-            + [VM((2 * LAYERS, D, F), bf16), VM((NU, 32, W), f32), VM((NU, 32, W), f32), VM((128, W), f32)]
+            + [VM((2 * LAYERS, D, F), bf16), VM((NU, 32, W), f32), VM((NU, 32, W), f32), VM((4, 128, W), f32)]
             + [VM((8, 128), f32), VM((32, W), f32)]
             + [DMA, DMA, DMA((8,)), DMA((8,)), DMA((2,)), DMA((2,)), DMA((2,)), DMA, DMA((Gather.N,))]
             + Gather.scratch()
@@ -722,12 +737,13 @@
             x, y, w_in, w_out,
             collective=1,
         )
-        new_in, new_out = call(
+        new_in, new_out, mean = call(
             place_kernel,
-            [S((LAYERS, D, F), f32), S((LAYERS, F, D), f32)],
-            [VM((8, D, W), f32), VM((8, D, W), f32), VM((8, W, D), f32)] + [DMA((8,))] * 4,
-            parts,
+            [S((LAYERS, D, F), f32), S((LAYERS, F, D), f32), S((1, 1), f32)],
+            [VM((8, D, W), f32), VM((8, D, W), f32), VM((8, W, D), f32), VM((8, 128), f32)] + [DMA((8,))] * 4 + [DMA],
+            parts, loss,
+            out_specs=[ANY, ANY, pl.BlockSpec(memory_space=pltpu.SMEM)],
         )
-        return new_in, new_out, (0.5 * jnp.sum(loss)) * (1.0 / (tokens * DEVICES * D))
+        return new_in, new_out, mean.reshape(())
 
     return jax.shard_map(step, mesh=mesh, in_specs=(spec, spec, P(), P()), out_specs=(P(), P(), P()), check_vma=False)

time: 541 us -> 531 us (0.982)
  Pallas kernels: 537 us -> 530 us
    pallas_call x2, Pallas kernels: 537 us -> 530 us  [call(): pl.pallas_call(lambda *refs: kernel(tokens, *refs), out_shape=outs, in_sp...]
where the time goes in v3:
time: 531 us
  Pallas kernels  530 us (100%)
    pallas_call x2, Pallas kernels, call(): pl.pallas_call(lambda *refs: kernel(tokens, *refs), out_shape=outs, in_sp...  530 us

profile of v3, /device:TPU:0, one launch (start us, length us, event | category | flops | bytes accessed | tf_op | source)
XLA Modules:
  0.0 531.0 jit_solution(11962115575847046444)
XLA Ops:
  0.6 506.4 %step_kernel.1 = (f32[32,2,512,256]{3,2,1,0:T(8,128)}, f32[8,128]{1,0:T(8,128)}, bf16[4,1568,512]{2,1,0:T(8,128)(2,1)}, bf16[3,1568,2048]{2,1,0:T(8,128)(2,1)}, bf16[3,1568,2048]{2,1,0:T(8,128)(2,1)}) custom-call(bf16[1568,512]{1,0:T(8,128)(2,1)} %bitcast.7, bf16[1568,512]{1,0:T(8,128)(2,1)} %bitcast.8, f32[4,512,2048]{2,1,0:T(8,128)} %refs_2_.1, ...), custom_call_target="tpu_custom_call" | custom-call | tf_op jit(solution)/shard_map/step_kernel/pallas_call | solution.py:714
  507.1 23.8 %place_kernel.1 = (f32[4,512,2048]{2,1,0:T(8,128)}, f32[4,2048,512]{2,1,0:T(8,128)}, f32[1,1]{1,0:T(1,128)}) custom-call(f32[32,2,512,256]{3,2,1,0:T(8,128)} %get-tuple-element.8.refs_0_, f32[8,128]{1,0:T(8,128)} %get-tuple-element.9.refs_1_), custom_call_target="tpu_custom_call" | custom-call | tf_op jit(solution)/shard_map/place_kernel/pallas_call | solution.py:714

commit v4 on v3

--- a/solution.py
+++ b/solution.py
@@ -21,7 +21,7 @@
 W = 256
 NU = 32
 ROWS = (512, 256, 128, 64, 32)
-VMEM_LIMIT = 62 * 2**20
+VMEM_LIMIT = 67_043_328
 
 ANY = pl.BlockSpec(memory_space=pl.ANY)
 DMA = pltpu.SemaphoreType.DMA
@@ -80,15 +80,14 @@
 
 
 class ReduceScatter:
-    NSD, ND, NA, N, LAG = 4, 8, 16, 8, 2
+    NSD, ND, NA, N, LAG = 8, 6, 16, 8, 2
     TICKS = NU + 4 * LAG
 
     @classmethod
     def scratch(cls):
         n = cls.N
         return [
-            pltpu.VMEM((cls.NSD, 512, W), f32),
-            pltpu.VMEM((cls.NA, 512, W), f32),
+            pltpu.VMEM((cls.NA + cls.NSD, 512, W), f32),
             pltpu.VMEM((cls.ND, 512, W), f32),
             pltpu.VMEM((n, 256, W), f32),
             pltpu.VMEM((n, 128, W), f32),
@@ -103,12 +102,12 @@
 
     def __init__(self, cube, refs):
         self.cube = cube
-        (self.out, self.acc, self.inc, r1, r2, r3, r4, self.dsend, self.drecv, self.ssem, self.rsem, self.credit) = refs
+        (self.acc, self.inc, r1, r2, r3, r4, self.dsend, self.drecv, self.ssem, self.rsem, self.credit) = refs
         self.recv = (r1, r2, r3, r4)
 
     def core_copy(self, k):
         return remote(
-            self.out.at[k % self.NSD],
+            self.acc.at[self.NA + k % self.NSD],
             self.inc.at[k % self.ND],
             self.dsend.at[k % self.NSD],
             self.drecv.at[k % self.ND],
@@ -256,9 +255,9 @@
 ):
     rows = tokens // 2
     cube = Cube()
-    scatter = ReduceScatter(cube, refs[:12])
-    norm_sum = Spread(cube, refs[12:16])
-    loss_sum = Spread(cube, refs[16:20])
+    scatter = ReduceScatter(cube, refs[:11])
+    norm_sum = Spread(cube, refs[11:15])
+    loss_sum = Spread(cube, refs[15:19])
     row = cube.keep[3]
     col = cube.core * HALF
     stage = scatter.acc
@@ -275,8 +274,11 @@
     def part(r):
         return pl.ds(aligned(r * rows, 16), rows)
 
+    def slot_a(l, j):
+        return (l % 2) * 16 + j
+
     def load_a(l, j):
-        return copy(win.at[l, :, pl.ds(aligned(j * W, W), W)], stage.at[j], sa.at[j])
+        return copy(win.at[l, :, pl.ds(aligned(j * W, W), W)], stage.at[slot_a(l, j)], sa.at[j])
 
     def load_b(l, j):
         return copy(
@@ -294,14 +296,14 @@
             load(l, j).wait()
 
     def round_a(l, j):
-        wts[2 * l, :, pl.ds(aligned(j * W, W), W)] = stage[j].astype(bf16)
+        wts[2 * l, :, pl.ds(aligned(j * W, W), W)] = stage[slot_a(l, j)].astype(bf16)
 
     def round_b(l, j):
         block = stage[8 + j].T.astype(bf16)
         wts[2 * l + 1, pl.ds(aligned((j % 2) * W, W), W), pl.ds(aligned((j // 2) * 512, 512), 512)] = block
 
     def keep_a(l, j):
-        shard[(LAYERS - 1 - l) * 8 + 4 + j] = stage[cube.core * 4 + j, pl.ds(aligned(row, 32), 32), :]
+        shard[(LAYERS - 1 - l) * 8 + 4 + j] = stage[slot_a(l, cube.core * 4 + j), pl.ds(aligned(row, 32), 32), :]
 
     def keep_b(l, j):
         slot = 8 + (cube.core * 2 + j // 2) * 2 + row // W
@@ -321,62 +323,50 @@
     copy_x = copy(x_in, h.at[0], sx)
     copy_y = copy(y_in, d, sy)
 
-    def forward(tick, before_in, before_out, beside_in, beside_out, whole):
+    def forward(tick, before_in, before_out, beside_in):
         def layer(l, carry):
             cur = l % 2
 
-            def wait_saves(r):
+            def half_in(r, carry):
                 @pl.when(l >= 1)
                 def _():
                     save_u(l - 1, r).wait()
-                    save_act(l - 1, r).wait()
-
-            def start_saves(r):
+
+                u[part(r), :] = dot(h[cur, part(r), :], wts[2 * l]).astype(bf16)
+                beside_in(l, r)
+
                 @pl.when(l < LAYERS - 1)
                 def _():
                     save_u(l, r).start()
-                    save_act(l, r).start()
-
-            def rows_in(r):
-                u[part(r), :] = dot(h[cur, part(r), :], wts[2 * l]).astype(bf16)
+
+                tick(4 * l + r)
+                return carry
+
+            def half_out(r, carry):
+                @pl.when(l >= 1)
+                def _():
+                    save_act(l - 1, r).wait()
+
                 a[part(r), :] = gelu(u[part(r), :]).astype(bf16)
-                beside_in(l, r)
-
-            def rows_out(r):
                 acc = dot(a[part(r), :], wts[2 * l + 1], 1, 1)
                 h[1 - cur, part(r), :] = (h[cur, part(r), :].astype(f32) + acc).astype(bf16)
-                beside_out(l, r)
-
-            def half_in(r, carry):
-                wait_saves(r)
-                rows_in(r)
-                start_saves(r)
-                tick(4 * l + r)
-                return carry
-
-            def half_out(r, carry):
-                rows_out(r)
+
+                @pl.when(l < LAYERS - 1)
+                def _():
+                    save_act(l, r).start()
+
                 tick(4 * l + 2 + r)
                 return carry
 
             before_in(l)
-            if whole:
-                for step in (wait_saves, rows_in, start_saves):
-                    for r in range(2):
-                        step(r)
-            else:
-                lax.fori_loop(0, 2, half_in, 0)
+            lax.fori_loop(0, 2, half_in, 0)
             before_out(l)
 
             @pl.when(l >= 1)
             def _():
                 save_h(l - 1).wait()
 
-            if whole:
-                for r in range(2):
-                    rows_out(r)
-            else:
-                lax.fori_loop(0, 2, half_out, 0)
+            lax.fori_loop(0, 2, half_out, 0)
 
             @pl.when(l < LAYERS - 1)
             def _():
@@ -404,8 +394,8 @@
             scatter.before_write(k)
             scatter.before_write(k + 1)
             value = dot(lhs[...], src[:, pl.ds(aligned(away + pair * 512, 512), 512)], 0, 0)
-            scatter.out[k % scatter.NSD] = value[:, :W]
-            scatter.out[(k + 1) % scatter.NSD] = value[:, W:]
+            scatter.acc[scatter.NA + k % scatter.NSD] = value[:, :W]
+            scatter.acc[scatter.NA + (k + 1) % scatter.NSD] = value[:, W:]
             scatter.push(k)
             scatter.push(k + 1)
             value = dot(lhs[...], src[:, pl.ds(aligned(own + pair * 512, 512), 512)], 0, 0)
@@ -502,17 +492,18 @@
     copy_x.start()
     start_all(load_a, 0)
     start_all(load_b, 0)
-    copy_y.start()
     lax.fori_loop(1, DEVICES, greet, 0)
     copy_x.wait()
     save_h(0).start()
 
     def round_first(j, carry):
         load_a(0, j).wait()
+        load_a(1, j).start()
         round_a(0, j)
         return carry
 
     lax.fori_loop(0, 8, round_first, 0)
+    copy_y.start()
     for j in range(4):
         keep_a(0, j)
 
@@ -521,28 +512,27 @@
 
         @pl.when(l < LAYERS - 1)
         def _():
-            start_all(load_a, l + 1)
+            wait_all(load_a, l + 1)
+
+        @pl.when(l < LAYERS - 2)
+        def _():
+            start_all(load_a, l + 2)
 
     def beside_in_1(l, r):
+        following = jnp.minimum(l + 1, LAYERS - 1)
         for j in range(4):
             round_b(l, r * 4 + j)
+            round_a(following, r * 4 + j)
         for j in range(2):
             keep_b(l, r * 2 + j)
+            keep_a(following, r * 2 + j)
 
     def before_out_1(l):
         @pl.when(l < LAYERS - 1)
         def _():
             start_all(load_b, l + 1)
-            wait_all(load_a, l + 1)
-
-    def beside_out_1(l, r):
-        following = jnp.minimum(l + 1, LAYERS - 1)
-        for j in range(4):
-            round_a(following, r * 4 + j)
-        for j in range(2):
-            keep_a(following, r * 2 + j)
-
-    forward(nothing, before_in_1, before_out_1, beside_in_1, beside_out_1, False)
+
+    forward(nothing, before_in_1, before_out_1, beside_in_1)
     for r in range(2):
         diff = h[0, part(r), :].astype(f32) - d[part(r), :].astype(f32)
         d[part(r), :] = (diff * inv_count).astype(bf16)
@@ -594,7 +584,7 @@
     lax.fori_loop(0, lead, first, 0)
     copy_x.wait()
     save_h(0).start()
-    forward(lambda t: weights.tick(lead + t), nothing, nothing, nothing, nothing, False)
+    forward(lambda t: weights.tick(lead + t), nothing, nothing, nothing)
     squares = jnp.zeros((1, D), f32)
     for r in range(2):
         diff = h[0, part(r), :].astype(f32) - d[part(r), :].astype(f32)

time: 531 us -> 530 us (level)
  no operation moved by 1% of the time
where the time goes in v4:
time: 530 us
  Pallas kernels  529 us (100%)
    pallas_call x2, Pallas kernels, call(): pl.pallas_call(lambda *refs: kernel(tokens, *refs), out_shape=outs, in_sp...  529 us

profile of v4, /device:TPU:0, one launch (start us, length us, event | category | flops | bytes accessed | tf_op | source)
XLA Modules:
  0.0 529.6 jit_solution(6234234691233069454)
XLA Ops:
  0.6 505.0 %step_kernel.1 = (f32[32,2,512,256]{3,2,1,0:T(8,128)}, f32[8,128]{1,0:T(8,128)}, bf16[4,1568,512]{2,1,0:T(8,128)(2,1)}, bf16[3,1568,2048]{2,1,0:T(8,128)(2,1)}, bf16[3,1568,2048]{2,1,0:T(8,128)(2,1)}) custom-call(bf16[1568,512]{1,0:T(8,128)(2,1)} %bitcast.7, bf16[1568,512]{1,0:T(8,128)(2,1)} %bitcast.8, f32[4,512,2048]{2,1,0:T(8,128)} %refs_2_.1, ...), custom_call_target="tpu_custom_call" | custom-call | tf_op jit(solution)/shard_map/step_kernel/pallas_call | solution.py:704
  505.6 23.8 %place_kernel.1 = (f32[4,512,2048]{2,1,0:T(8,128)}, f32[4,2048,512]{2,1,0:T(8,128)}, f32[1,1]{1,0:T(1,128)}) custom-call(f32[32,2,512,256]{3,2,1,0:T(8,128)} %get-tuple-element.8.refs_0_, f32[8,128]{1,0:T(8,128)} %get-tuple-element.9.refs_1_), custom_call_target="tpu_custom_call" | custom-call | tf_op jit(solution)/shard_map/place_kernel/pallas_call | solution.py:704
